TPU v7x, 256 devices: a whole 4x4x8 slice. The times are simulated.
256 devices in a mesh: gx: 8 (over y, core), gy: 4 (over x), gz: 8 (over z).
Axes of the slice: x: 4, y: 4, z: 8, core: 2. Of those that a mesh axis runs over, the one named last changes fastest.
Arguments:
- density: float32 [128, 64, 8192], P('gx', 'gy', 'gz'), may hold values from -19 to 19
Outputs:
- potential: float32 [128, 64, 8192], P('gx', 'gy', 'gz')
- coulomb: float32 [64, 64], replicated
All inputs are finite; a program needn't handle non-finite values.
Results may differ from a plain program's by a relative error of at most 0.000057.
Values sent between devices are 32-bit elements; how exact they have to be, the bound alone decides.
A program may use at most 64 MiB of HBM per device.

v0:
```python
import functools

import jax
import jax.numpy as jnp
from jax import lax
from jax.sharding import Mesh
from jax.sharding import PartitionSpec as P

PAIRS = 64
LEVELS = 6
COARSE_SWEEPS = 8
GX = ("gx_0", "gx_1")
GX_GY_GZ = ("gx_0", "gx_1", "gy", "gz")


OMEGA = 2.0 / 3.0


def extended_2(x, sides, width):
    for axis, dim in sides:
        size, length = (lax.axis_size(axis), x.shape[dim])
        up = [(i, (i + 1) % size) for i in range(size - 1)]
        down = [(j, i) for i, j in up]
        last = lax.slice_in_dim(x, length - width, length, axis=dim)
        initial = lax.slice_in_dim(x, 0, width, axis=dim)
        before = lax.ppermute(last, axis, up)
        after = lax.ppermute(initial, axis, down)
        x = jnp.concatenate([before, x, after], axis=dim)
    return x


def by_axis(x, axes):
    return functools.reduce(lax.psum, axes, x)


def neighbours(padded):
    total = padded[2:, 1:-1, 1:-1] + padded[:-2, 1:-1, 1:-1]
    total = total + padded[1:-1, 2:, 1:-1] + padded[1:-1, :-2, 1:-1]
    return total + padded[1:-1, 1:-1, 2:] + padded[1:-1, 1:-1, :-2]


def apply_inner(padded, factor):
    return factor * (6.0 * padded[1:-1, 1:-1, 1:-1] - neighbours(padded))


def sweep_inner(padded, source, factor):
    return padded[1:-1, 1:-1, 1:-1] + OMEGA * (source - apply_inner(padded, factor)) / (
        6.0 * factor
    )


def zero_rim(current):
    return jnp.pad(current, ((1, 1), (1, 1), (1, 1), (0, 0)))


def restrict(residual):
    size_x, size_y, size_z, count = residual.shape
    grouped = residual.reshape(size_x // 2, 2, size_y // 2, 2, size_z // 2, 2, count)
    return jnp.mean(grouped, axis=(1, 3, 5))


def prolong(correction):
    return jnp.repeat(jnp.repeat(jnp.repeat(correction, 2, axis=0), 2, axis=1), 2, axis=2)


def global_cycle(source, grid_level):
    factor = 0.25 ** (grid_level - 1)
    current = OMEGA * source / (6.0 * factor)
    if grid_level == LEVELS:
        for repeat_no in range(COARSE_SWEEPS - 1):
            current = sweep_inner(zero_rim(current), source, factor)
        return current
    current = sweep_inner(zero_rim(current), source, factor)
    residual = source - apply_inner(zero_rim(current), factor)
    current = current + prolong(global_cycle(restrict(residual), grid_level + 1))
    for repeat_no in range(2):
        current = sweep_inner(zero_rim(current), source, factor)
    return current


def arrange(stacked, block_shape):
    size_x, size_y, size_z, count = block_shape
    devs_x, devs_y, devs_z = (lax.axis_size(GX), lax.axis_size("gy"), lax.axis_size("gz"))
    grouped = stacked.reshape(devs_x, devs_y, devs_z, size_x, size_y, size_z, count)
    grouped = grouped.transpose(0, 3, 1, 4, 2, 5, 6)
    return grouped.reshape(devs_x * size_x, devs_y * size_y, devs_z * size_z, count)


def own_block(gathered, block_shape):
    size_x, size_y, size_z, count = block_shape
    starts = (
        lax.axis_index(GX) * size_x,
        lax.axis_index("gy") * size_y,
        lax.axis_index("gz") * size_z,
        jnp.int32(0),
    )
    return lax.dynamic_slice(gathered, starts, block_shape)


def edge_mask(length, where, devices):
    position = jnp.arange(length + 2, dtype=jnp.int32) - 1 + where * length
    return (position >= 0) & (position < length * devices)


def inside_mask(block_shape):
    mask_x = edge_mask(block_shape[0], lax.axis_index(GX), lax.axis_size(GX))
    mask_y = edge_mask(block_shape[1], lax.axis_index("gy"), lax.axis_size("gy"))
    mask_z = edge_mask(block_shape[2], lax.axis_index("gz"), lax.axis_size("gz"))
    joined = mask_x[:, None, None] & mask_y[None, :, None] & mask_z[None, None, :]
    return joined[..., None].astype(jnp.float32)


def double_sweep(current, source, factor):
    count = current.shape[3]
    extended = extended_2(
        jnp.concatenate([current, source], axis=3), ((GX, 0), ("gy", 1), ("gz", 2)), 2
    )
    source_wide = extended[1:-1, 1:-1, 1:-1, count:]
    swept = sweep_inner(extended[..., :count], source_wide, factor) * inside_mask(current.shape)
    return swept


def distributed(source, grid_level):
    factor = 0.25 ** (grid_level - 1)
    if grid_level == LEVELS - 2:
        stacked = lax.all_gather(source[None], GX_GY_GZ, axis=0, tiled=True)
        return own_block(global_cycle(arrange(stacked, source.shape), grid_level), source.shape)
    current = OMEGA * source / (6.0 * factor)
    swept = double_sweep(current, source, factor)
    residual = source - apply_inner(swept, factor)
    current = swept[1:-1, 1:-1, 1:-1]
    current = current + prolong(distributed(restrict(residual), grid_level + 1))
    current = sweep_inner(double_sweep(current, source, factor), source, factor)
    return current


def local(density):
    cells_x, cells_y, merged = density.shape
    cells_z = merged // PAIRS
    cells = density.reshape(cells_x, cells_y, cells_z, PAIRS)
    solved = distributed(cells, 1)
    partial_block = jnp.dot(
        cells.reshape(-1, PAIRS).T,
        solved.reshape(-1, PAIRS),
        precision=lax.Precision.HIGHEST,
        preferred_element_type=jnp.float32,
    )
    summed = by_axis(partial_block, GX_GY_GZ)
    total_cells = (
        cells_x * cells_y * cells_z * lax.axis_size(GX) * lax.axis_size("gy") * lax.axis_size("gz")
    )
    coulomb = summed * (4.0 / total_cells)
    return (solved.reshape(cells_x, cells_y, merged), coulomb)


def solution(mesh):
    finer = Mesh(
        mesh.devices.reshape(4, 2, mesh.shape["gy"], mesh.shape["gz"]), ("gx_0", "gx_1", "gy", "gz")
    )
    placed = (P(GX, "gy", "gz"),)
    return jax.shard_map(
        local, mesh=finer, in_specs=placed, out_specs=(P(GX, "gy", "gz"), P()), check_vma=False
    )
```

profile of v0, /device:TPU:2, one launch (start us, length us, event | category | flops | bytes accessed | tf_op | source)
XLA Modules:
  0.0 400.2 jit_solution(6967951721887709520)
XLA Ops:
  32.4 5.9 %collective-permute-done.4 = f32[20,20,2,128]{3,2,1,0:T(2,128)S(1)} collective-permute-done((f32[20,20,2,128]{3,2,1,0:T(2,128)S(1)}, f32[20,20,2,128]{3,2,1,0:T(2,128)S(1)}, u32[]{:S(2)}, u32[]{:S(2)}) %collective-permute-start.4) | collective-permute-done | bytes 409632 | tf_op jit(solution)/shard_map/ppermute | solution.py:26
  38.3 4.5 %collective-permute-done.5 = f32[20,20,2,128]{3,2,1,0:T(2,128)S(1)} collective-permute-done((f32[20,20,2,128]{3,2,1,0:T(2,128)S(1)}, f32[20,20,2,128]{3,2,1,0:T(2,128)S(1)}, u32[]{:S(2)}, u32[]{:S(2)}) %collective-permute-start.5) | collective-permute-done | bytes 409632 | tf_op jit(solution)/shard_map/ppermute | solution.py:27
  46.1 8.6 %fusion.23 = f32[18,18,18,64]{3,2,1,0:T(8,128)S(1)} fusion(f32[16,16,16,64]{3,2,1,0:T(8,128)S(1)} %reshape.265, f32[20,20,2,128]{3,2,1,0:T(2,128)S(1)} %collective-permute-done.4, f32[20,2,16,128]{3,2,1,0:T(8,128)S(1)} %collective-permute-done.3, f32[20,2,16,128]{3,2,1,0:T(8,128)S(1)} %collective-permute-done.2, ...), kind=kLoop, calls=%fused_computation.53 | loop fusion | flops 8584704 | bytes 14570272 | tf_op jit(solution)/shard_map/mul | solution.py:119
  61.1 4.0 collective-permute-start.6
  66.4 8.3 %collective-permute-done.7 = f32[2,8,8,128]{3,2,1,0:T(8,128)S(1)} collective-permute-done((f32[2,8,8,128]{3,2,1,0:T(8,128)S(1)}, f32[2,8,8,128]{3,2,1,0:T(8,128)S(1)}, u32[]{:S(2)}, u32[]{:S(2)}) %collective-permute-start.7) | collective-permute-done | bytes 65568 | tf_op jit(solution)/shard_map/ppermute | solution.py:27
  93.3 5.5 %collective-permute-done.11 = f32[12,12,2,128]{3,2,1,0:T(2,128)} collective-permute-done((f32[12,12,2,128]{3,2,1,0:T(2,128)}, f32[12,12,2,128]{3,2,1,0:T(2,128)}, u32[]{:S(2)}, u32[]{:S(2)}) %collective-permute-start.11) | collective-permute-done | bytes 147488 | tf_op jit(solution)/shard_map/ppermute | solution.py:27
  107.6 4.0 %collective-permute-done.13 = f32[2,4,4,128]{3,2,1,0:T(4,128)S(1)} collective-permute-done((f32[2,4,4,128]{3,2,1,0:T(4,128)S(1)}, f32[2,4,4,128]{3,2,1,0:T(4,128)S(1)}, u32[]{:S(2)}, u32[]{:S(2)}) %collective-permute-start.13) | collective-permute-done | bytes 16416 | tf_op jit(solution)/shard_map/ppermute | solution.py:27
  113.7 3.9 collective-permute-start.15
  119.6 4.9 %collective-permute-start.16 = (f32[8,8,2,128]{3,2,1,0:T(2,128)S(1)}, f32[8,8,2,128]{3,2,1,0:T(2,128)S(1)}, u32[]{:S(2)}, u32[]{:S(2)}) collective-permute-start(f32[8,8,2,128]{3,2,1,0:T(2,128)S(1)} %get-tuple-element.43), channel_id=1, source_target_pairs={{0,1},{1,2},{2,3},{3,4},{4,5},{5,6},{6,7},{8,9},{9,10},{10,11},{11... | collective-permute-start | bytes 196616 | tf_op jit(solution)/shard_map/ppermute | solution.py:26
  126.6 4.7 %collective-permute-done.17 = f32[8,8,2,128]{3,2,1,0:T(2,128)S(1)} collective-permute-done((f32[8,8,2,128]{3,2,1,0:T(2,128)S(1)}, f32[8,8,2,128]{3,2,1,0:T(2,128)S(1)}, u32[]{:S(2)}, u32[]{:S(2)}) %collective-permute-start.17) | collective-permute-done | bytes 65568 | tf_op jit(solution)/shard_map/ppermute | solution.py:27
  132.3 64.3 %all-gather = f32[512,2,2,64]{3,2,1,0:T(2,128)S(1)} all-gather(f32[2,2,2,64]{3,2,1,0:T(2,128)S(1)} %broadcast_multiply_fusion.10), channel_id=2, replica_groups=mesh['gx_0'=4,'gx_1'=2,'gy'=4,'gz'=8] {'gx_0','gx_1','gy','gz'}, dimensions={0}, use_global_device_ids=true | all-gather | bytes 526336 | tf_op jit(solution)/shard_map/all_gather | solution.py:126
  226.2 4.6 %collective-permute-done.23 = f32[8,8,2,128]{3,2,1,0:T(2,128)S(1)} collective-permute-done((f32[8,8,2,128]{3,2,1,0:T(2,128)S(1)}, f32[8,8,2,128]{3,2,1,0:T(2,128)S(1)}, u32[]{:S(2)}, u32[]{:S(2)}) %collective-permute-start.23) | collective-permute-done | bytes 65568 | tf_op jit(solution)/shard_map/ppermute | solution.py:27
  238.8 3.9 collective-permute-start.26
  245.3 3.9 collective-permute-done.27
  249.5 3.9 collective-permute-start.28
  257.1 4.7 %collective-permute-done.29 = f32[12,12,2,128]{3,2,1,0:T(2,128)S(1)} collective-permute-done((f32[12,12,2,128]{3,2,1,0:T(2,128)S(1)}, f32[12,12,2,128]{3,2,1,0:T(2,128)S(1)}, u32[]{:S(2)}, u32[]{:S(2)}) %collective-permute-start.29) | collective-permute-done | bytes 147488 | tf_op jit(solution)/shard_map/ppermute | solution.py:27
  287.4 5.4 %collective-permute-start.34 = (f32[20,20,2,128]{3,2,1,0:T(2,128)}, f32[20,20,2,128]{3,2,1,0:T(2,128)}, u32[]{:S(2)}, u32[]{:S(2)}) collective-permute-start(f32[20,20,2,128]{3,2,1,0:T(2,128)} %get-tuple-element.15), channel_id=1, source_target_pairs={{0,1},{1,2},{2,3},{3,4},{4,5},{5,6},{6,7},{8,9},{9,10},{10,11},{11... | collective-permute-start | bytes 1228808 | tf_op jit(solution)/shard_map/ppermute | solution.py:26
  299.8 5.4 %collective-permute-done.35 = f32[20,20,2,128]{3,2,1,0:T(2,128)} collective-permute-done((f32[20,20,2,128]{3,2,1,0:T(2,128)}, f32[20,20,2,128]{3,2,1,0:T(2,128)}, u32[]{:S(2)}, u32[]{:S(2)}) %collective-permute-start.35) | collective-permute-done | bytes 409632 | tf_op jit(solution)/shard_map/ppermute | solution.py:27
  305.2 4.6 %fusion.11 = f32[20,20,20,128]{3,2,1,0:T(8,128)S(1)} fusion(f32[16,16,16,64]{3,2,1,0:T(8,128)S(1)} %reshape.265, f32[20,20,2,128]{3,2,1,0:T(2,128)} %collective-permute-done.35, f32[20,2,16,128]{3,2,1,0:T(8,128)S(1)} %collective-permute-done.33, f32[2,16,16,128]{3,2,1,0:T(8,128)S(1)} %collective-permute-done.31, f32[16,16,16,64]{3,2,1,0:T(8,128)} %copy-done.4, ...), kind=kLoop, calls=%fused_computation.13 | loop fusion | flops 7168000 | bytes 8192000 | tf_op jit(solution)/shard_map/concatenate | solution.py:28
  309.8 9.5 %fusion.35 = f32[18,18,18,64]{3,2,1,0:T(8,128)S(1)} fusion(f32[16,16,16,64]{3,2,1,0:T(8,128)S(1)} %reshape.265, f32[20,20,2,128]{3,2,1,0:T(2,128)} %collective-permute-done.34, f32[20,2,16,128]{3,2,1,0:T(8,128)S(1)} %collective-permute-done.33, f32[20,2,16,128]{3,2,1,0:T(8,128)S(1)} %collective-permute-done.32, ...), kind=kLoop, calls=%fused_computation.65 | loop fusion | flops 8584704 | bytes 14570272 | tf_op jit(solution)/shard_map/mul | solution.py:119
  325.3 5.2 %convolution_bitcast_fusion = f32[64,64]{0,1:T(8,128)S(1)} fusion(f32[4096,64]{1,0:T(8,128)S(1)} %bitcast.36, f32[4096,64]{1,0:T(8,128)} %reshape_reshape.3), kind=kOutput, calls=%fused_computation.156 | convolution fusion | flops 201326592 | bytes 2113536 | tf_op jit(solution)/shard_map/dot_general | solution.py:142
  330.4 23.2 %psum.28 = f32[64,64]{0,1:T(8,128)S(1)} all-reduce(f32[64,64]{0,1:T(8,128)S(1)} %convolution_bitcast_fusion), channel_id=1, replica_groups=mesh['gx_0'=4,'gx_1'=2,'gy'=4,'gz'=8] {'gx_0'}, use_global_device_ids=true, to_apply=%region_5.6 | all-reduce | flops 4096 | bytes 32768 | tf_op jit(solution)/shard_map/psum | solution.py:33
  357.1 14.3 %psum.30 = f32[64,64]{0,1:T(8,128)S(1)} all-reduce(f32[64,64]{0,1:T(8,128)S(1)} %psum.29), channel_id=1, replica_groups=mesh['gx_0'=4,'gx_1'=2,'gy'=4,'gz'=8] {'gy'}, use_global_device_ids=true, to_apply=%region_7.8 | all-reduce | flops 4096 | bytes 32768 | tf_op jit(solution)/shard_map/psum | solution.py:33
  371.4 28.0 %psum.31 = f32[64,64]{0,1:T(8,128)S(1)} all-reduce(f32[64,64]{0,1:T(8,128)S(1)} %psum.30), channel_id=1, replica_groups=mesh['gx_0'=4,'gx_1'=2,'gy'=4,'gz'=8] {'gz'}, use_global_device_ids=true, to_apply=%region_8.9 | all-reduce | flops 4096 | bytes 32768 | tf_op jit(solution)/shard_map/psum | solution.py:33
  (221 shorter events, 162.9 us)
Async XLA Ops:
  13.6 9.0 %collective-permute-start.2 = (f32[20,2,16,128]{3,2,1,0:T(8,128)S(1)}, f32[20,2,16,128]{3,2,1,0:T(8,128)S(1)}, u32[]{:S(2)}, u32[]{:S(2)}) collective-permute-start(f32[20,2,16,128]{3,2,1,0:T(8,128)S(1)} %get-tuple-element.20), channel_id=1, source_target_pairs={{0,8},{8,16},{16,24},{1,9},{9,17},{17,25},{2,10},{10,18},{18,26},{... | collective-permute-start | bytes 983048 | tf_op jit(solution)/shard_map/ppermute | solution.py:26
  17.0 9.0 %collective-permute-start.3 = (f32[20,2,16,128]{3,2,1,0:T(8,128)S(1)}, f32[20,2,16,128]{3,2,1,0:T(8,128)S(1)}, u32[]{:S(2)}, u32[]{:S(2)}) collective-permute-start(f32[20,2,16,128]{3,2,1,0:T(8,128)S(1)} %get-tuple-element.21), channel_id=1, source_target_pairs={{8,0},{16,8},{24,16},{9,1},{17,9},{25,17},{10,2},{18,10},{26,18},{... | collective-permute-start | bytes 983048 | tf_op jit(solution)/shard_map/ppermute | solution.py:27
  27.0 11.3 %collective-permute-start.4 = (f32[20,20,2,128]{3,2,1,0:T(2,128)S(1)}, f32[20,20,2,128]{3,2,1,0:T(2,128)S(1)}, u32[]{:S(2)}, u32[]{:S(2)}) collective-permute-start(f32[20,20,2,128]{3,2,1,0:T(2,128)S(1)} %get-tuple-element.17), channel_id=1, source_target_pairs={{0,1},{1,2},{2,3},{3,4},{4,5},{5,6},{6,7},{8,9},{9,10},{10,11},{11... | collective-permute-start | bytes 1228808 | tf_op jit(solution)/shard_map/ppermute | solution.py:26
  30.8 12.0 %collective-permute-start.5 = (f32[20,20,2,128]{3,2,1,0:T(2,128)S(1)}, f32[20,20,2,128]{3,2,1,0:T(2,128)S(1)}, u32[]{:S(2)}, u32[]{:S(2)}) collective-permute-start(f32[20,20,2,128]{3,2,1,0:T(2,128)S(1)} %get-tuple-element.16), channel_id=1, source_target_pairs={{1,0},{2,1},{3,2},{4,3},{5,4},{6,5},{7,6},{9,8},{10,9},{11,10},{12... | collective-permute-start | bytes 1228808 | tf_op jit(solution)/shard_map/ppermute | solution.py:27
  65.0 9.7 %collective-permute-start.7 = (f32[2,8,8,128]{3,2,1,0:T(8,128)S(1)}, f32[2,8,8,128]{3,2,1,0:T(8,128)S(1)}, u32[]{:S(2)}, u32[]{:S(2)}) collective-permute-start(f32[2,8,8,128]{3,2,1,0:T(8,128)S(1)} %get-tuple-element.10), channel_id=1, source_target_pairs={{32,0},{64,32},{96,64},{128,96},{160,128},{192,160},{224,192},{33,... | collective-permute-start | bytes 196616 | tf_op jit(solution)/shard_map/ppermute | solution.py:27
  74.9 6.5 %collective-permute-start.8 = (f32[12,2,8,128]{3,2,1,0:T(8,128)S(1)}, f32[12,2,8,128]{3,2,1,0:T(8,128)S(1)}, u32[]{:S(2)}, u32[]{:S(2)}) collective-permute-start(f32[12,2,8,128]{3,2,1,0:T(8,128)S(1)} %get-tuple-element.33), channel_id=1, source_target_pairs={{0,8},{8,16},{16,24},{1,9},{9,17},{17,25},{2,10},{10,18},{18,26},{... | collective-permute-start | bytes 294920 | tf_op jit(solution)/shard_map/ppermute | solution.py:26
  78.0 6.5 %collective-permute-start.9 = (f32[12,2,8,128]{3,2,1,0:T(8,128)S(1)}, f32[12,2,8,128]{3,2,1,0:T(8,128)S(1)}, u32[]{:S(2)}, u32[]{:S(2)}) collective-permute-start(f32[12,2,8,128]{3,2,1,0:T(8,128)S(1)} %get-tuple-element.34), channel_id=1, source_target_pairs={{8,0},{16,8},{24,16},{9,1},{17,9},{25,17},{10,2},{18,10},{26,18},{... | collective-permute-start | bytes 294920 | tf_op jit(solution)/shard_map/ppermute | solution.py:27
  85.5 7.8 %collective-permute-start.10 = (f32[12,12,2,128]{3,2,1,0:T(2,128)}, f32[12,12,2,128]{3,2,1,0:T(2,128)S(1)}, u32[]{:S(2)}, u32[]{:S(2)}) collective-permute-start(f32[12,12,2,128]{3,2,1,0:T(2,128)} %get-tuple-element.30), channel_id=1, source_target_pairs={{0,1},{1,2},{2,3},{3,4},{4,5},{5,6},{6,7},{8,9},{9,10},{10,11},{11... | collective-permute-start | bytes 442376 | tf_op jit(solution)/shard_map/ppermute | solution.py:26
  89.3 9.5 %collective-permute-start.11 = (f32[12,12,2,128]{3,2,1,0:T(2,128)}, f32[12,12,2,128]{3,2,1,0:T(2,128)}, u32[]{:S(2)}, u32[]{:S(2)}) collective-permute-start(f32[12,12,2,128]{3,2,1,0:T(2,128)} %get-tuple-element.29), channel_id=1, source_target_pairs={{1,0},{2,1},{3,2},{4,3},{5,4},{6,5},{7,6},{9,8},{10,9},{11,10},{12... | collective-permute-start | bytes 442376 | tf_op jit(solution)/shard_map/ppermute | solution.py:27
  111.7 5.9 %collective-permute-start.14 = (f32[8,2,4,128]{3,2,1,0:T(4,128)S(1)}, f32[8,2,4,128]{3,2,1,0:T(4,128)S(1)}, u32[]{:S(2)}, u32[]{:S(2)}) collective-permute-start(f32[8,2,4,128]{3,2,1,0:T(4,128)S(1)} %get-tuple-element.48), channel_id=1, source_target_pairs={{0,8},{8,16},{16,24},{1,9},{9,17},{17,25},{2,10},{10,18},{18,26},{... | collective-permute-start | bytes 98312 | tf_op jit(solution)/shard_map/ppermute | solution.py:26
  113.7 5.8 %collective-permute-start.15 = (f32[8,2,4,128]{3,2,1,0:T(4,128)S(1)}, f32[8,2,4,128]{3,2,1,0:T(4,128)S(1)}, u32[]{:S(2)}, u32[]{:S(2)}) collective-permute-start(f32[8,2,4,128]{3,2,1,0:T(4,128)S(1)} %get-tuple-element.49), channel_id=1, source_target_pairs={{8,0},{16,8},{24,16},{9,1},{17,9},{25,17},{10,2},{18,10},{26,18},{... | collective-permute-start | bytes 98312 | tf_op jit(solution)/shard_map/ppermute | solution.py:27
  119.6 7.0 %collective-permute-start.16 = (f32[8,8,2,128]{3,2,1,0:T(2,128)S(1)}, f32[8,8,2,128]{3,2,1,0:T(2,128)S(1)}, u32[]{:S(2)}, u32[]{:S(2)}) collective-permute-start(f32[8,8,2,128]{3,2,1,0:T(2,128)S(1)} %get-tuple-element.43), channel_id=1, source_target_pairs={{0,1},{1,2},{2,3},{3,4},{4,5},{5,6},{6,7},{8,9},{9,10},{10,11},{11... | collective-permute-start | bytes 196616 | tf_op jit(solution)/shard_map/ppermute | solution.py:26
  124.5 6.8 %collective-permute-start.17 = (f32[8,8,2,128]{3,2,1,0:T(2,128)S(1)}, f32[8,8,2,128]{3,2,1,0:T(2,128)S(1)}, u32[]{:S(2)}, u32[]{:S(2)}) collective-permute-start(f32[8,8,2,128]{3,2,1,0:T(2,128)S(1)} %get-tuple-element.42), channel_id=1, source_target_pairs={{1,0},{2,1},{3,2},{4,3},{5,4},{6,5},{7,6},{9,8},{10,9},{11,10},{12... | collective-permute-start | bytes 196616 | tf_op jit(solution)/shard_map/ppermute | solution.py:27
  213.3 5.9 %collective-permute-start.20 = (f32[8,2,4,128]{3,2,1,0:T(4,128)S(1)}, f32[8,2,4,128]{3,2,1,0:T(4,128)S(1)}, u32[]{:S(2)}, u32[]{:S(2)}) collective-permute-start(f32[8,2,4,128]{3,2,1,0:T(4,128)S(1)} %get-tuple-element.44), channel_id=1, source_target_pairs={{0,8},{8,16},{16,24},{1,9},{9,17},{17,25},{2,10},{10,18},{18,26},{... | collective-permute-start | bytes 98312 | tf_op jit(solution)/shard_map/ppermute | solution.py:26
  215.2 6.4 %collective-permute-start.21 = (f32[8,2,4,128]{3,2,1,0:T(4,128)S(1)}, f32[8,2,4,128]{3,2,1,0:T(4,128)S(1)}, u32[]{:S(2)}, u32[]{:S(2)}) collective-permute-start(f32[8,2,4,128]{3,2,1,0:T(4,128)S(1)} %get-tuple-element.45), channel_id=1, source_target_pairs={{8,0},{16,8},{24,16},{9,1},{17,9},{25,17},{10,2},{18,10},{26,18},{... | collective-permute-start | bytes 98312 | tf_op jit(solution)/shard_map/ppermute | solution.py:27
  224.3 6.5 %collective-permute-start.23 = (f32[8,8,2,128]{3,2,1,0:T(2,128)S(1)}, f32[8,8,2,128]{3,2,1,0:T(2,128)S(1)}, u32[]{:S(2)}, u32[]{:S(2)}) collective-permute-start(f32[8,8,2,128]{3,2,1,0:T(2,128)S(1)} %get-tuple-element.40), channel_id=1, source_target_pairs={{1,0},{2,1},{3,2},{4,3},{5,4},{6,5},{7,6},{9,8},{10,9},{11,10},{12... | collective-permute-start | bytes 196616 | tf_op jit(solution)/shard_map/ppermute | solution.py:27
  238.8 6.5 %collective-permute-start.26 = (f32[12,2,8,128]{3,2,1,0:T(8,128)S(1)}, f32[12,2,8,128]{3,2,1,0:T(8,128)S(1)}, u32[]{:S(2)}, u32[]{:S(2)}) collective-permute-start(f32[12,2,8,128]{3,2,1,0:T(8,128)S(1)} %get-tuple-element.31), channel_id=1, source_target_pairs={{0,8},{8,16},{16,24},{1,9},{9,17},{17,25},{2,10},{10,18},{18,26},{... | collective-permute-start | bytes 294920 | tf_op jit(solution)/shard_map/ppermute | solution.py:26
  242.7 6.5 %collective-permute-start.27 = (f32[12,2,8,128]{3,2,1,0:T(8,128)S(1)}, f32[12,2,8,128]{3,2,1,0:T(8,128)S(1)}, u32[]{:S(2)}, u32[]{:S(2)}) collective-permute-start(f32[12,2,8,128]{3,2,1,0:T(8,128)S(1)} %get-tuple-element.32), channel_id=1, source_target_pairs={{8,0},{16,8},{24,16},{9,1},{17,9},{25,17},{10,2},{18,10},{26,18},{... | collective-permute-start | bytes 294920 | tf_op jit(solution)/shard_map/ppermute | solution.py:27
  249.5 7.6 %collective-permute-start.28 = (f32[12,12,2,128]{3,2,1,0:T(2,128)S(1)}, f32[12,12,2,128]{3,2,1,0:T(2,128)S(1)}, u32[]{:S(2)}, u32[]{:S(2)}) collective-permute-start(f32[12,12,2,128]{3,2,1,0:T(2,128)S(1)} %get-tuple-element.28), channel_id=1, source_target_pairs={{0,1},{1,2},{2,3},{3,4},{4,5},{5,6},{6,7},{8,9},{9,10},{10,11},{11... | collective-permute-start | bytes 442376 | tf_op jit(solution)/shard_map/ppermute | solution.py:26
  253.4 8.4 %collective-permute-start.29 = (f32[12,12,2,128]{3,2,1,0:T(2,128)S(1)}, f32[12,12,2,128]{3,2,1,0:T(2,128)S(1)}, u32[]{:S(2)}, u32[]{:S(2)}) collective-permute-start(f32[12,12,2,128]{3,2,1,0:T(2,128)S(1)} %get-tuple-element.27), channel_id=1, source_target_pairs={{1,0},{2,1},{3,2},{4,3},{5,4},{6,5},{7,6},{9,8},{10,9},{11,10},{12... | collective-permute-start | bytes 442376 | tf_op jit(solution)/shard_map/ppermute | solution.py:27
  274.1 9.0 %collective-permute-start.32 = (f32[20,2,16,128]{3,2,1,0:T(8,128)S(1)}, f32[20,2,16,128]{3,2,1,0:T(8,128)S(1)}, u32[]{:S(2)}, u32[]{:S(2)}) collective-permute-start(f32[20,2,16,128]{3,2,1,0:T(8,128)S(1)} %get-tuple-element.18), channel_id=1, source_target_pairs={{0,8},{8,16},{16,24},{1,9},{9,17},{17,25},{2,10},{10,18},{18,26},{... | collective-permute-start | bytes 983048 | tf_op jit(solution)/shard_map/ppermute | solution.py:26
  276.6 9.0 %collective-permute-start.33 = (f32[20,2,16,128]{3,2,1,0:T(8,128)S(1)}, f32[20,2,16,128]{3,2,1,0:T(8,128)S(1)}, u32[]{:S(2)}, u32[]{:S(2)}) collective-permute-start(f32[20,2,16,128]{3,2,1,0:T(8,128)S(1)} %get-tuple-element.19), channel_id=1, source_target_pairs={{8,0},{16,8},{24,16},{9,1},{17,9},{25,17},{10,2},{18,10},{26,18},{... | collective-permute-start | bytes 983048 | tf_op jit(solution)/shard_map/ppermute | solution.py:27
  287.4 12.4 %collective-permute-start.34 = (f32[20,20,2,128]{3,2,1,0:T(2,128)}, f32[20,20,2,128]{3,2,1,0:T(2,128)}, u32[]{:S(2)}, u32[]{:S(2)}) collective-permute-start(f32[20,20,2,128]{3,2,1,0:T(2,128)} %get-tuple-element.15), channel_id=1, source_target_pairs={{0,1},{1,2},{2,3},{3,4},{4,5},{5,6},{6,7},{8,9},{9,10},{10,11},{11... | collective-permute-start | bytes 1228808 | tf_op jit(solution)/shard_map/ppermute | solution.py:26
  292.7 12.5 %collective-permute-start.35 = (f32[20,20,2,128]{3,2,1,0:T(2,128)}, f32[20,20,2,128]{3,2,1,0:T(2,128)}, u32[]{:S(2)}, u32[]{:S(2)}) collective-permute-start(f32[20,20,2,128]{3,2,1,0:T(2,128)} %get-tuple-element.14), channel_id=1, source_target_pairs={{1,0},{2,1},{3,2},{4,3},{5,4},{6,5},{7,6},{9,8},{10,9},{11,10},{12... | collective-permute-start | bytes 1228808 | tf_op jit(solution)/shard_map/ppermute | solution.py:27
  (38 other events, 558.1 us)
where the time goes:
time: 402 us; the launch traced here: 400 us
  blocking collectives  133 us (33%)
  waiting for transfers between devices  93.3 us (23%)
  starting transfers between devices  88.2 us (22%)
  other arithmetic  60 us (15%)
  local copies, waits for them, and re-layouts  18.3 us (5%)
  matrix products  5.15 us (1%)
    ppermute x18, waiting for transfers between devices, extended_2(): after = lax.ppermute(initial, axis, down)  71 us
    psum x4, blocking collectives, by_axis(): return functools.reduce(lax.psum, axes, x)  69 us
    all_gather x1, blocking collectives, distributed(): stacked = lax.all_gather(source[None], GX_GY_GZ, axis=0, tiled=True)  64.3 us
    ppermute x18, starting transfers between devices, extended_2(): before = lax.ppermute(last, axis, up)  53.9 us
    ppermute x18, starting transfers between devices, extended_2(): after = lax.ppermute(initial, axis, down)  34.3 us
    mul x6, other arithmetic, double_sweep(): sweep_inner(extended[..., :count], source_wide, factor)  22.4 us
    ppermute x18, waiting for transfers between devices, extended_2(): before = lax.ppermute(last, axis, up)  22.3 us
    concatenate x18, other arithmetic, extended_2(): x = jnp.concatenate([before, x, after], axis=dim)  14.7 us
  transfers between devices with their start and end apart: 36, of which 28 were waited for; matrix products, arithmetic and copies ran while one was open for 1% of the time, Pallas kernels for 0%

commit v1 on v0

v1 whole, which is shorter than its diff:
```python
import functools

import jax
import jax.numpy as jnp
from jax import lax
from jax.experimental import pallas as pl
from jax.experimental.pallas import tpu as pltpu
from jax.sharding import PartitionSpec as P

PAIRS = 64
LANES = 128
YO = 8
CENTRE = 1.0 / 3.0
SIDE = 1.0 / 9.0
MESH = pl.DeviceIdType.MESH
F32 = jnp.float32


def tau(level):
    return (1.0 / 9.0) * 4.0 ** (level - 1)


def low_lanes():
    return lax.broadcasted_iota(jnp.int32, (1, LANES), 1) < PAIRS


def swap(v):
    return pltpu.roll(v, PAIRS, v.ndim - 1)


def smooth(a, t, x, row, n):
    own = a[t, x, pl.ds(row, n), :]
    total = a[t, x, pl.ds(row - 1, n), :] + a[t, x, pl.ds(row + 1, n), :]
    total = total + (a[t, x - 1, pl.ds(row, n), :] + a[t, x + 1, pl.ds(row, n), :])
    beyond = jnp.where(low_lanes(), a[t + 1, x, pl.ds(row, n), :], a[t - 1, x, pl.ds(row, n), :])
    total = total + swap(own + beyond)
    return own * CENTRE + total * SIDE


def loop(n, body, unroll_below=3):
    if n < unroll_below:
        for i in range(n):
            body(i)
    else:
        lax.fori_loop(0, n, lambda i, c: (body(i), c)[1], 0)


def restrict_rows(r, t, x, rows):
    s = r[t, x, pl.ds(YO, rows, stride=2), :] + r[t, x, pl.ds(YO + 1, rows, stride=2), :]
    s = s + (r[t, x + 1, pl.ds(YO, rows, stride=2), :] + r[t, x + 1, pl.ds(YO + 1, rows, stride=2), :])
    return s + swap(s)


def coarse_cell(r, tc, xc, rows):
    even = restrict_rows(r, 2 * tc + 1, 2 * xc + 1, rows)
    odd = restrict_rows(r, 2 * tc + 2, 2 * xc + 1, rows)
    return jnp.where(low_lanes(), even, odd) * 0.125


def zero_faces(a, tiles, planes, rows, inside=None):
    flat = jnp.zeros((rows, LANES), F32)
    line = jnp.zeros((1, LANES), F32)

    def plane(x):
        def body(t):
            a[t + 1, x, pl.ds(YO, rows), :] = flat

        return lambda: loop(tiles, body)

    def edge(row):
        def body(t):
            for x in range(1, planes + 1):
                a[t + 1, x, pl.ds(row, 1), :] = line

        return lambda: loop(tiles, body)

    def tile(t):
        def fill():
            for x in range(1, planes + 1):
                a[t, x, pl.ds(YO, rows), :] = flat

        return fill

    fills = (plane(0), plane(planes + 1), edge(YO - 1), edge(YO + rows), tile(0), tile(tiles + 1))
    for i, fill in enumerate(fills):
        if inside is None:
            fill()
        else:
            pl.when(jnp.logical_not(inside[i]))(fill)


def dot_t(a, b):
    return lax.dot_general(
        a, b, (((0,), (0,)), ((), ())), precision=lax.Precision.HIGHEST, preferred_element_type=F32
    )


def kernel(
    nums, dens, pot, coul,
    f1, h1, r1, w1, f2, h2, r2, w2, f3, h3, r3, w3,
    f4, h4, r4, q4, k4, c4, f5, h5, r5, q5, k5, c5, f6, a6, b6,
    q3, k3, c3, q2, k2, c2, q1, k1, out,
    acc, acc4, cp, ca, cs, cb, ct, cc,
    send, recv, io,
):
    ngx, ngy, ngz = nums
    gx, gy, gz = (lax.axis_index(a) for a in ("gx", "gy", "gz"))
    me = (gx, gy, gz)
    sizes = (ngx, ngy, ngz)
    names = ("gx", "gy", "gz")
    chip, core = gx // 2, gx % 2
    chips = ngx // 2
    counter = [0]
    sent = []

    def has(offset):
        cond = None
        for pos, size, d in zip(me, sizes, offset):
            if d == 0:
                continue
            this = pos + d >= 0 if d < 0 else pos + d < size
            cond = this if cond is None else cond & this
        return cond

    def when(cond, fn):
        if cond is None:
            fn()
        else:
            pl.when(cond)(fn)

    def opposite(offset):
        return tuple(-d for d in offset)

    def near(offset):
        return {n: p + d for n, p, d in zip(names, me, offset) if d != 0}

    class Msg:
        def __init__(self, src, dst, device, cond_send, cond_recv):
            i = counter[0]
            counter[0] += 1
            self.copy = pltpu.make_async_remote_copy(
                src_ref=src, dst_ref=dst, send_sem=send.at[i], recv_sem=recv.at[i], device_id=device, device_id_type=MESH
            )
            self.cond_send, self.cond_recv = cond_send, cond_recv

        def start(self):
            when(self.cond_send, self.copy.start)
            sent.append(self)

        def wait(self):
            when(self.cond_recv, self.copy.wait_recv)

        def drain(self):
            when(self.cond_send, self.copy.wait_send)

    def start(msgs):
        for m in msgs:
            m.start()
        return msgs

    def wait(msgs):
        for m in msgs:
            m.wait()

    def faces(a, tiles, planes, rows):
        ts, xs, ys = pl.ds(1, tiles), pl.ds(1, planes), pl.ds(YO, rows)
        spec = [
            ((-1, 0, 0), (ts, pl.ds(1, 1), ys), (ts, pl.ds(planes + 1, 1), ys)),
            ((1, 0, 0), (ts, pl.ds(planes, 1), ys), (ts, pl.ds(0, 1), ys)),
            ((0, -1, 0), (ts, xs, pl.ds(YO, 1)), (ts, xs, pl.ds(YO + rows, 1))),
            ((0, 1, 0), (ts, xs, pl.ds(YO + rows - 1, 1)), (ts, xs, pl.ds(YO - 1, 1))),
            ((0, 0, -1), (pl.ds(1, 1), xs, ys), (pl.ds(tiles + 1, 1), xs, ys)),
            ((0, 0, 1), (pl.ds(tiles, 1), xs, ys), (pl.ds(0, 1), xs, ys)),
        ]
        return start(
            [Msg(a.at[src], a.at[dst], near(o), has(o), has(opposite(o))) for o, src, dst in spec]
        )

    def rims(a, tiles, planes, rows, width, corners):
        def part(d, size, w, first):
            if d == 0:
                return pl.ds(first, size), pl.ds(first, size)
            if d < 0:
                return pl.ds(first, w), pl.ds(first + size, w)
            return pl.ds(first + size - w, w), pl.ds(first - w, w)

        msgs = []
        for dx in (-1, 0, 1):
            for dy in (-1, 0, 1):
                for dz in (-1, 0, 1):
                    order = abs(dx) + abs(dy) + abs(dz)
                    if order == 0 or (order == 3 and not corners):
                        continue
                    o = (dx, dy, dz)
                    z_src, z_dst = part(dz, tiles, 1, 1)
                    x_src, x_dst = part(dx, planes, width, width)
                    y_src, y_dst = part(dy, rows, width, width)
                    msgs.append(
                        (order, Msg(a.at[z_src, x_src, y_src], a.at[z_dst, x_dst, y_dst], near(o), has(o), has(opposite(o))))
                    )
        msgs.sort(key=lambda m: -m[0])
        return start([m for _, m in msgs])

    loads = [
        pltpu.make_async_copy(
            dens.at[:, :, pl.ds(t * LANES, LANES)], f1.at[t + 1, pl.ds(1, 16), pl.ds(YO, 16)], io.at[t]
        )
        for t in range(8)
    ]
    for c in loads:
        c.start()
    w2[...] = jnp.zeros(w2.shape, F32)
    w3[...] = jnp.zeros(w3.shape, F32)
    barrier = pltpu.get_barrier_semaphore()
    expected = jnp.int32(0)
    for dx in (-1, 0, 1):
        for dy in (-1, 0, 1):
            for dz in (-1, 0, 1):
                o = (dx, dy, dz)
                if o == (0, 0, 0):
                    continue
                cond = has(o)

                @pl.when(cond)
                def _(o=o):
                    pl.semaphore_signal(barrier, inc=1, device_id=near(o), device_id_type=MESH)

                expected = expected + cond.astype(jnp.int32)
    for d in range(1, ngz):
        pl.semaphore_signal(barrier, inc=1, device_id={"gz": lax.rem(gz + d, ngz)}, device_id_type=MESH)
    others = [(dx, dy) for dx in range(ngx) for dy in range(ngy) if (dx, dy) != (0, 0)]

    def other(dx, dy):
        return {"gx": lax.rem(gx + dx, ngx), "gy": lax.rem(gy + dy, ngy)}

    for dx, dy in others:
        pl.semaphore_signal(barrier, inc=1, device_id=other(dx, dy), device_id_type=MESH)
    expected = expected + (ngz - 1 + len(others))

    near_side = [has(o) for o in ((-1, 0, 0), (1, 0, 0), (0, -1, 0), (0, 1, 0), (0, 0, -1), (0, 0, 1))]
    for a in (f1, h1, r1):
        zero_faces(a, 8, 16, 16, near_side)
    for a in (f2, h2, r2):
        zero_faces(a, 4, 8, 8, near_side)
    for a in (f3, h3, r3):
        zero_faces(a, 2, 4, 4, near_side)
    x4, y4, t4 = 2 * ngx, 2 * ngy, ngz
    for a in (f4, h4, r4, q4, k4):
        zero_faces(a, t4, x4, y4)
    c4[...] = jnp.zeros(c4.shape, F32)
    for a in (f5, h5, r5, q5, k5):
        zero_faces(a, t4 // 2, x4 // 2, y4 // 2)
    for a in (f6, a6, b6):
        zero_faces(a, t4 // 4, x4 // 4, y4 // 4)
    acc[...] = jnp.zeros(acc.shape, F32)
    acc4[...] = jnp.zeros(acc4.shape, F32)

    for c in loads:
        c.wait()
    pl.semaphore_wait(barrier, expected)

    def apply(dst, src, tiles, planes, rows):
        def body(t):
            for x in range(1, planes + 1):
                dst[t + 1, x, pl.ds(YO, rows), :] = smooth(src, t + 1, x, YO, rows)

        loop(tiles, body)

    def restrict(dst, r, tiles, planes, rows):
        def body(tc):
            for xc in range(planes):
                dst[tc + 1, xc + 1, pl.ds(YO, rows), :] = coarse_cell(r, tc, xc, rows)

        loop(tiles, body)

    def collect(w, f, h, r, tiles, planes, rows, x0, y0, level):
        def body(t):
            for x in range(planes):
                at = (t + 1, x + 1, pl.ds(YO, rows), slice(None))
                v = f[at] + h[at] + r[at] + smooth(r, t + 1, x + 1, YO, rows)
                w[t + (x0 > 0), x + x0, pl.ds(y0, rows), :] = v * tau(level)

        loop(tiles, body)

    def energy(f, h, r, tiles, planes, rows, level):
        padded = -(-rows // 8) * 8
        keep = lax.broadcasted_iota(jnp.int32, (1, padded, 1), 1) < rows

        def body(t):
            at = (t + 1, pl.ds(1, planes), pl.ds(YO, padded), slice(None))
            vf, vh, vr = f[at], h[at], r[at]
            if padded != rows:
                vf, vh, vr = (jnp.where(keep, v, 0.0) for v in (vf, vh, vr))
            vf, vh, vr = (v.reshape(planes * padded, LANES) for v in (vf, vh, vr))
            acc[...] += (dot_t(vf, vf + vh) + dot_t(vh, vh + vr)) * (tau(level) * 8.0 ** (level - 1))

        loop(tiles, body)

    wait(faces(f1, 8, 16, 16))
    apply(h1, f1, 8, 16, 16)
    wait(faces(h1, 8, 16, 16))
    apply(r1, h1, 8, 16, 16)
    restrict(f2, r1, 4, 8, 8)
    m_f2 = faces(f2, 4, 8, 8)
    m_r1 = faces(r1, 8, 16, 16)
    energy(f1, h1, r1, 8, 16, 16, 1)
    wait(m_f2)
    apply(h2, f2, 4, 8, 8)
    m_h2 = faces(h2, 4, 8, 8)
    wait(m_r1)
    collect(w1, f1, h1, r1, 8, 16, 16, 0, 0, 1)
    wait(m_h2)
    apply(r2, h2, 4, 8, 8)
    restrict(f3, r2, 2, 4, 4)
    m_f3 = faces(f3, 2, 4, 4)
    m_r2 = faces(r2, 4, 8, 8)
    energy(f2, h2, r2, 4, 8, 8, 2)
    wait(m_f3)
    apply(h3, f3, 2, 4, 4)
    m_h3 = faces(h3, 2, 4, 4)
    wait(m_r2)
    collect(w2, f2, h2, r2, 4, 8, 8, 1, 1, 2)
    wait(m_h3)
    apply(r3, h3, 2, 4, 4)

    own_x, own_y = pl.ds(2 * gx + 1, 2), pl.ds(YO + 2 * gy, 2)
    for x in range(2):
        f4[gz + 1, 2 * gx + 1 + x, own_y, :] = coarse_cell(r3, 0, x, 2)
    all_t = pl.ds(1, t4)
    block = f4.at[pl.ds(gz + 1, 1), own_x, own_y]
    m_z = start(
        [Msg(block, block, {"gz": lax.rem(gz + d, ngz)}, None, None) for d in range(1, ngz)]
    )
    m_r3 = faces(r3, 2, 4, 4)
    m_w2 = rims(w2, 4, 8, 8, 1, False)
    wait(m_r3)
    energy(f3, h3, r3, 2, 4, 4, 3)
    collect(w3, f3, h3, r3, 2, 4, 4, 2, 2, 3)
    m_w3 = rims(w3, 2, 4, 4, 2, True)
    piece = 32 // ngz
    square = acc[0:PAIRS, :] + swap(acc[PAIRS:, :])
    packed = jnp.where(low_lanes(), square[0:32, :], swap(square[32:64, :]))
    for k in range(ngz):
        cp[k] = packed[k * piece : (k + 1) * piece, :]
    m_ca = []
    for d in range(1, ngz):
        to = lax.rem(gz + d, ngz)
        m_ca.append(Msg(cp.at[to], ca.at[gz], {"gz": to}, None, None))
    start(m_ca)
    ca[gz] = cp[gz]

    wait(m_z)
    line = f4.at[all_t, own_x, own_y]
    m_p = []
    for dx in range(chips):
        for dy in range(ngy):
            if (dx, dy) != (0, 0):
                to = {"gx": lax.rem(chip + dx, chips) * 2 + core, "gy": lax.rem(gy + dy, ngy)}
                m_p.append(Msg(line, line, to, None, None))
    start(m_p)
    wait(m_ca)
    total = ca[0]
    for k in range(1, ngz):
        total = total + ca[k]
    cs[...] = total
    slot = gx * ngy + gy
    cb[slot] = total
    m_cb = start([Msg(cs, cb.at[slot], other(dx, dy), None, None) for dx, dy in others])
    wait(m_p)
    m_c = []
    for j in range(chips):
        part = f4.at[all_t, pl.ds(2 * (2 * j + core) + 1, 2), pl.ds(YO, y4)]
        m_c.append(Msg(part, part, {"gx": 2 * chip + 1 - core}, None, None))
    start(m_c)
    wait(m_c)

    apply(h4, f4, t4, x4, y4)
    apply(r4, h4, t4, x4, y4)
    x5, y5, t5 = x4 // 2, y4 // 2, t4 // 2
    x6, y6, t6 = x5 // 2, y5 // 2, t5 // 2
    restrict(f5, r4, t5, x5, y5)
    apply(h5, f5, t5, x5, y5)
    apply(r5, h5, t5, x5, y5)
    restrict(f6, r5, t6, x6, y6)
    for t in range(1, t6 + 1):
        for x in range(1, x6 + 1):
            at = (t, x, pl.ds(YO, y6), slice(None))
            v = f6[at] * tau(6)
            f6[at] = v
            a6[at] = v
    now, later = a6, b6
    for _ in range(7):
        for t in range(1, t6 + 1):
            for x in range(1, x6 + 1):
                at = (t, x, pl.ds(YO, y6), slice(None))
                later[at] = f6[at] + smooth(now, t, x, YO, y6)
        now, later = later, now

    def prolong(dst, value, tile, x, row, rows, which=(0, 1)):
        turned = swap(value)
        halves = (jnp.where(low_lanes(), value, turned), jnp.where(low_lanes(), turned, value))
        for k in which:
            for i in range(2):
                for j in range(2):
                    dst[tile + k, x + i, pl.ds(row + j, rows, stride=2), :] = halves[k]

    def coarse_up(c, f, h, r, q, k, coarse, first, tiles, planes, rows, level, pad):
        def spread(t):
            for x in range(planes // 2):
                value = coarse[t + 1, x + first, pl.ds(YO, rows // 2), :]
                prolong(q, value, 2 * t + 1, 2 * x + 1, YO, rows // 2)

        loop(tiles // 2, spread)
        apply(k, q, tiles, planes, rows)

        def body(t):
            for x in range(1, planes + 1):
                at = (t + 1, x, pl.ds(YO, rows), slice(None))
                v = (f[at] + h[at] + r[at] + smooth(r, t + 1, x, YO, rows)) * tau(level)
                c[t + 1, x + pad, pl.ds(YO, rows), :] = v + smooth(k, t + 1, x, YO, rows)

        loop(tiles, body)

    coarse_up(c5, f5, h5, r5, q5, k5, now, 1, t5, x5, y5, 5, 0)
    coarse_up(c4, f4, h4, r4, q4, k4, c5, 1, t4, x4, y4, 4, 1)

    wait(m_cb)
    total = cb[0]
    for k in range(1, ngx * ngy):
        total = total + cb[k]
    ct[...] = total
    cc[gz] = total
    m_cc = start(
        [Msg(ct, cc.at[gz], {"gz": lax.rem(gz + d, ngz)}, None, None) for d in range(1, ngz)]
    )

    inside = [
        tuple(c.astype(F32) for c in (p > 0, p < n - 1)) for p, n in zip(me, sizes)
    ]

    def row_mask(n, first, own):
        row = lax.broadcasted_iota(jnp.int32, (n, LANES), 0)
        one = jnp.ones((n, LANES), F32)
        return jnp.where(row < first, one * inside[1][0], jnp.where(row >= first + own, one * inside[1][1], one))

    def side(axis, i, own):
        return inside[axis][0] if i < 0 else inside[axis][1] if i >= own else None

    def masked(v, mask, *scalars):
        v = v * mask
        for s in scalars:
            if s is not None:
                v = v * s
        return v

    wait(m_w3)
    for j in range(3):
        for i in range(6):
            value = c4[gz + j, 2 * gx + i, pl.ds(YO - 2 + 2 * gy, 6), :]
            prolong(q3, value, 1 + 2 * j, 2 * i, 0, 6)
    mask = row_mask(10, 3, 4)
    for t in range(-2, 4):
        for x in range(-3, 7):
            v = smooth(q3, t + 3, x + 4, 1, 10)
            k3[t + 3, x + 4, pl.ds(1, 10), :] = masked(v, mask, side(2, t, 2), side(0, x, 4))
    mask = row_mask(8, 2, 4)
    for t in range(-1, 3):
        for x in range(-2, 6):
            v = w3[t + 1, x + 2, pl.ds(0, 8), :] + smooth(k3, t + 3, x + 4, 2, 8)
            prolong(q2, masked(v, mask, side(2, t, 2), side(0, x, 4)), 2 * t + 3, 2 * x + 4, 0, 8)

    wait(m_w2)
    mask = row_mask(12, 2, 8)
    for t in range(-1, 5):
        for x in range(-2, 10):
            v = smooth(q2, t + 3, x + 4, 2, 12)
            k2[t + 3, x + 4, pl.ds(2, 12), :] = masked(v, mask, side(2, t, 4), side(0, x, 8))
    mask = row_mask(10, 1, 8)
    for t in range(-1, 5):
        for x in range(-1, 9):
            v = w2[t + 1, x + 1, pl.ds(0, 10), :] + smooth(k2, t + 3, x + 4, 3, 10)
            which = (1,) if t < 0 else (0,) if t >= 4 else (0, 1)
            prolong(q1, masked(v, mask, side(2, t, 4), side(0, x, 8)), 2 * t + 2, 2 * x + 2, 0, 10, which)

    mask = row_mask(18, 1, 16)

    def rim_tile(t):
        for x in range(0, 16):
            v = smooth(q1, t + 2, x + 2, 1, 18)
            k1[t + 2, x + 2, pl.ds(1, 18), :] = masked(v, mask, side(2, t, 8))

    def own_tile(t):
        for x in range(-1, 17):
            v = smooth(q1, t + 2, x + 2, 1, 18)
            k1[t + 2, x + 2, pl.ds(1, 18), :] = masked(v, mask, side(0, x, 16))

    rim_tile(-1)
    rim_tile(8)
    loop(8, own_tile)

    def last(t):
        for x in range(16):
            out[t, x] = w1[t, x] + smooth(k1, t + 2, x + 2, 2, 16)

    loop(8, last)
    stores = [
        pltpu.make_async_copy(out.at[t], pot.at[:, :, pl.ds(t * LANES, LANES)], io.at[t]) for t in range(8)
    ]
    for c in stores:
        c.start()

    padded = -(-y4 // 8) * 8
    keep = lax.broadcasted_iota(jnp.int32, (1, padded, 1), 1) < y4

    def level_4(t):
        vf = f4[t + 1, pl.ds(1, x4), pl.ds(YO, padded), :]
        vc = c4[t + 1, pl.ds(2, x4), pl.ds(YO, padded), :]
        if padded != y4:
            vf, vc = (jnp.where(keep, v, 0.0) for v in (vf, vc))
        acc4[...] += dot_t(vf.reshape(x4 * padded, LANES), vc.reshape(x4 * padded, LANES))

    loop(t4, level_4)
    coarse_part = (acc4[0:PAIRS, :] + swap(acc4[PAIRS:, :])) * 512.0
    wait(m_cc)
    packed = jnp.concatenate([cc[k] for k in range(ngz)], axis=0)
    scale = 4.0 / (ngx * ngy * ngz * 16 * 16 * 16)
    coul[0:32, :] = ((packed + coarse_part[0:32, :]) * scale)[:, :PAIRS]
    coul[32:64, :] = ((swap(packed) + coarse_part[32:64, :]) * scale)[:, :PAIRS]

    for c in stores:
        c.wait()
    for m in sent:
        m.drain()


def local(nums, density):
    ngx, ngy, ngz = nums
    piece = 32 // ngz

    def field(t, x, y):
        return pltpu.VMEM((t, x, y, LANES), F32)

    def level(t, x, y):
        return field(t + 2, x + 2, YO + -(-(y + 1) // 8) * 8)

    t4, x4, y4 = ngz, 2 * ngx, 2 * ngy
    l1, l2, l3 = level(8, 16, 16), level(4, 8, 8), level(2, 4, 4)
    l4, l5, l6 = (level(t4 // s, x4 // s, y4 // s) for s in (1, 2, 4))
    c4 = field(t4 + 2, x4 + 4, 24)
    scratch = [l1, l1, l1, field(8, 16, 16), l2, l2, l2, field(6, 10, 16), l3, l3, l3, field(4, 8, 8)]
    scratch += [l4, l4, l4, l4, l4, c4, l5, l5, l5, l5, l5, l5, l6, l6, l6]
    scratch += [field(8, 12, 16), field(8, 12, 16), field(1, 1, 8), field(10, 16, 16), field(10, 16, 16), field(1, 1, 8)]
    scratch += [field(12, 20, 24), field(12, 20, 24), field(8, 16, 16)]
    square = pltpu.VMEM((LANES, LANES), F32)
    row = pltpu.VMEM((piece, LANES), F32)
    scratch += [square, square, pltpu.VMEM((ngz, piece, LANES), F32), pltpu.VMEM((ngz, piece, LANES), F32), row]
    scratch += [pltpu.VMEM((ngx * ngy, piece, LANES), F32), row, pltpu.VMEM((ngz, piece, LANES), F32)]
    messages = 54 + 18 + 26 + 3 * (ngz - 1) + (ngx // 2 * ngy - 1) + (ngx * ngy - 1) + ngx // 2
    scratch += [pltpu.SemaphoreType.DMA((messages,)), pltpu.SemaphoreType.DMA((messages,)), pltpu.SemaphoreType.DMA((8,))]
    return pl.pallas_call(
        functools.partial(kernel, nums),
        out_shape=(
            jax.ShapeDtypeStruct(density.shape, F32),
            jax.ShapeDtypeStruct((PAIRS, PAIRS), F32),
        ),
        in_specs=[pl.BlockSpec(memory_space=pl.ANY)],
        out_specs=(pl.BlockSpec(memory_space=pl.ANY), pl.BlockSpec(memory_space=pltpu.VMEM)),
        scratch_shapes=scratch,
        compiler_params=pltpu.CompilerParams(
            collective_id=0, has_side_effects=True, vmem_limit_bytes=60_000_000
        ),
        name="cycle",
    )(density)


def solution(mesh):
    nums = tuple(mesh.shape[a] for a in ("gx", "gy", "gz"))
    placed = P("gx", "gy", "gz")
    return jax.shard_map(
        functools.partial(local, nums), mesh=mesh, in_specs=(placed,), out_specs=(placed, P()), check_vma=False
    )
```

time: 402 us -> 72.8 us (0.18)
  the two profiles are of different devices: /device:TPU:2 before, /device:TPU:1 now
where the time goes in v1:
time: 72.8 us; the launch traced here: 72.7 us
  Pallas kernels  69.1 us (95%)
  local copies, waits for them, and re-layouts  2.93 us (4%)
    pallas_call x1, Pallas kernels, local(): pl.pallas_call(functools.partial(kernel, nums), out_shape=(jax.ShapeDtype...  69.1 us
    unnamed x4, local copies, waits for them, and re-layouts  2.93 us

profile of v1, /device:TPU:1, one launch (start us, length us, event | category | flops | bytes accessed | tf_op | source)
XLA Modules:
  0.0 72.7 jit_solution(11819128290345732353)
XLA Ops:
  0.6 69.1 %cycle.1 = (f32[16,16,1024]{2,1,0:T(8,128)}, f32[64,64]{1,0:T(8,128)}) custom-call(f32[16,16,1024]{2,1,0:T(8,128)} %dens.1), custom_call_target="tpu_custom_call" | custom-call | tf_op jit(solution)/shard_map/cycle/pallas_call | solution.py:560
  69.7 0.0 copy-start
  69.8 2.3 %copy.5 = f32[16,16,1024]{2,1,0:T(8,128)} copy(f32[16,16,1024]{2,1,0:T(8,128)} %get-tuple-element.4) | data formatting | bytes 2097152
  72.1 0.0 copy-done
  72.1 0.6 copy.6
Async XLA Ops:
  69.7 2.3 %copy-start = (f32[64,64]{1,0:T(8,128)S(1)}, f32[64,64]{1,0:T(8,128)}, u32[]{:S(2)}) copy-start(f32[64,64]{1,0:T(8,128)} %get-tuple-element.5) | copy-start | bytes 49156

commit v2 on v1

--- a/solution.py
+++ b/solution.py
@@ -57,42 +57,35 @@
     return jnp.where(low_lanes(), even, odd) * 0.125
 
 
-def zero_faces(a, tiles, planes, rows, inside=None):
+def zero_faces(a, tiles, planes, rows):
     flat = jnp.zeros((rows, LANES), F32)
     line = jnp.zeros((1, LANES), F32)
 
-    def plane(x):
-        def body(t):
-            a[t + 1, x, pl.ds(YO, rows), :] = flat
-
-        return lambda: loop(tiles, body)
-
-    def edge(row):
-        def body(t):
-            for x in range(1, planes + 1):
-                a[t + 1, x, pl.ds(row, 1), :] = line
-
-        return lambda: loop(tiles, body)
-
-    def tile(t):
-        def fill():
-            for x in range(1, planes + 1):
-                a[t, x, pl.ds(YO, rows), :] = flat
-
-        return fill
-
-    fills = (plane(0), plane(planes + 1), edge(YO - 1), edge(YO + rows), tile(0), tile(tiles + 1))
-    for i, fill in enumerate(fills):
-        if inside is None:
-            fill()
-        else:
-            pl.when(jnp.logical_not(inside[i]))(fill)
+    def body(t):
+        a[t + 1, 0, pl.ds(YO, rows), :] = flat
+        a[t + 1, planes + 1, pl.ds(YO, rows), :] = flat
+        for x in range(1, planes + 1):
+            a[t + 1, x, pl.ds(YO - 1, 1), :] = line
+            a[t + 1, x, pl.ds(YO + rows, 1), :] = line
+
+    loop(tiles, body)
+    for x in range(1, planes + 1):
+        a[0, x, pl.ds(YO, rows), :] = flat
+        a[tiles + 1, x, pl.ds(YO, rows), :] = flat
+
+
+def halves(v):
+    high = v.astype(jnp.bfloat16)
+    return high, (v - high.astype(F32)).astype(jnp.bfloat16)
 
 
 def dot_t(a, b):
-    return lax.dot_general(
-        a, b, (((0,), (0,)), ((), ())), precision=lax.Precision.HIGHEST, preferred_element_type=F32
-    )
+    (ah, al), (bh, bl) = halves(a), halves(b)
+
+    def dot(u, v):
+        return lax.dot_general(u, v, (((0,), (0,)), ((), ())), preferred_element_type=F32)
+
+    return dot(ah, bh) + (dot(ah, bl) + dot(al, bh))
 
 
 def kernel(
@@ -162,48 +155,56 @@
         for m in msgs:
             m.wait()
 
-    def faces(a, tiles, planes, rows):
-        ts, xs, ys = pl.ds(1, tiles), pl.ds(1, planes), pl.ds(YO, rows)
-        spec = [
-            ((-1, 0, 0), (ts, pl.ds(1, 1), ys), (ts, pl.ds(planes + 1, 1), ys)),
-            ((1, 0, 0), (ts, pl.ds(planes, 1), ys), (ts, pl.ds(0, 1), ys)),
-            ((0, -1, 0), (ts, xs, pl.ds(YO, 1)), (ts, xs, pl.ds(YO + rows, 1))),
-            ((0, 1, 0), (ts, xs, pl.ds(YO + rows - 1, 1)), (ts, xs, pl.ds(YO - 1, 1))),
-            ((0, 0, -1), (pl.ds(1, 1), xs, ys), (pl.ds(tiles + 1, 1), xs, ys)),
-            ((0, 0, 1), (pl.ds(tiles, 1), xs, ys), (pl.ds(0, 1), xs, ys)),
-        ]
+    offsets = [
+        (dx, dy, dz) for dx in (-1, 0, 1) for dy in (-1, 0, 1) for dz in (-1, 0, 1) if (dx, dy, dz) != (0, 0, 0)
+    ]
+    offsets.sort(key=lambda o: -sum(abs(d) for d in o))
+
+    def order(o):
+        return sum(abs(d) for d in o)
+
+    def rim(own, first, widths):
+        regions = []
+        for o in offsets:
+            if order(o) not in widths:
+                continue
+            src, dst = [], []
+            for axis, size, start_at, width in zip((2, 0, 1), own, first, (1, widths[order(o)], widths[order(o)])):
+                d = o[axis]
+                if d == 0:
+                    src.append(pl.ds(start_at, size))
+                    dst.append(pl.ds(start_at, size))
+                elif d < 0:
+                    src.append(pl.ds(start_at, width))
+                    dst.append(pl.ds(start_at + size, width))
+                else:
+                    src.append(pl.ds(start_at + size - width, width))
+                    dst.append(pl.ds(start_at - width, width))
+            regions.append((o, tuple(src), tuple(dst)))
+        return regions
+
+    def exchange(a, own, first, widths):
         return start(
-            [Msg(a.at[src], a.at[dst], near(o), has(o), has(opposite(o))) for o, src, dst in spec]
+            [
+                Msg(a.at[src], a.at[dst], near(o), has(o), has(opposite(o)))
+                for o, src, dst in rim(own, first, widths)
+            ]
         )
 
-    def rims(a, tiles, planes, rows, width, corners):
-        def part(d, size, w, first):
-            if d == 0:
-                return pl.ds(first, size), pl.ds(first, size)
-            if d < 0:
-                return pl.ds(first, w), pl.ds(first + size, w)
-            return pl.ds(first + size - w, w), pl.ds(first - w, w)
-
-        msgs = []
-        for dx in (-1, 0, 1):
-            for dy in (-1, 0, 1):
-                for dz in (-1, 0, 1):
-                    order = abs(dx) + abs(dy) + abs(dz)
-                    if order == 0 or (order == 3 and not corners):
-                        continue
-                    o = (dx, dy, dz)
-                    z_src, z_dst = part(dz, tiles, 1, 1)
-                    x_src, x_dst = part(dx, planes, width, width)
-                    y_src, y_dst = part(dy, rows, width, width)
-                    msgs.append(
-                        (order, Msg(a.at[z_src, x_src, y_src], a.at[z_dst, x_dst, y_dst], near(o), has(o), has(opposite(o))))
-                    )
-        msgs.sort(key=lambda m: -m[0])
-        return start([m for _, m in msgs])
+    def clear_outside(a, own, first, widths):
+        for o, _, dst in rim(own, first, widths):
+
+            @pl.when(jnp.logical_not(has(opposite(o))))
+            def _(dst=dst):
+                a[dst + (slice(None),)] = jnp.zeros(tuple(d.size for d in dst) + (LANES,), F32)
+
+    own_1, own_2, own_3 = (8, 16, 16), (4, 8, 8), (2, 4, 4)
+    wide = dict(first=(2, 2, YO), widths={1: 2, 2: 1})
+    thin = dict(first=(1, 1, YO), widths={1: 1})
 
     loads = [
         pltpu.make_async_copy(
-            dens.at[:, :, pl.ds(t * LANES, LANES)], f1.at[t + 1, pl.ds(1, 16), pl.ds(YO, 16)], io.at[t]
+            dens.at[:, :, pl.ds(t * LANES, LANES)], f1.at[t + 2, pl.ds(2, 16), pl.ds(YO, 16)], io.at[t]
         )
         for t in range(8)
     ]
@@ -213,19 +214,14 @@
     w3[...] = jnp.zeros(w3.shape, F32)
     barrier = pltpu.get_barrier_semaphore()
     expected = jnp.int32(0)
-    for dx in (-1, 0, 1):
-        for dy in (-1, 0, 1):
-            for dz in (-1, 0, 1):
-                o = (dx, dy, dz)
-                if o == (0, 0, 0):
-                    continue
-                cond = has(o)
-
-                @pl.when(cond)
-                def _(o=o):
-                    pl.semaphore_signal(barrier, inc=1, device_id=near(o), device_id_type=MESH)
-
-                expected = expected + cond.astype(jnp.int32)
+    for o in offsets:
+        cond = has(o)
+
+        @pl.when(cond)
+        def _(o=o):
+            pl.semaphore_signal(barrier, inc=1, device_id=near(o), device_id_type=MESH)
+
+        expected = expected + cond.astype(jnp.int32)
     for d in range(1, ngz):
         pl.semaphore_signal(barrier, inc=1, device_id={"gz": lax.rem(gz + d, ngz)}, device_id_type=MESH)
     others = [(dx, dy) for dx in range(ngx) for dy in range(ngy) if (dx, dy) != (0, 0)]
@@ -237,27 +233,60 @@
         pl.semaphore_signal(barrier, inc=1, device_id=other(dx, dy), device_id_type=MESH)
     expected = expected + (ngz - 1 + len(others))
 
-    near_side = [has(o) for o in ((-1, 0, 0), (1, 0, 0), (0, -1, 0), (0, 1, 0), (0, 0, -1), (0, 0, 1))]
-    for a in (f1, h1, r1):
-        zero_faces(a, 8, 16, 16, near_side)
-    for a in (f2, h2, r2):
-        zero_faces(a, 4, 8, 8, near_side)
-    for a in (f3, h3, r3):
-        zero_faces(a, 2, 4, 4, near_side)
+    clear_outside(f1, own_1, **wide)
+    for c in loads:
+        c.wait()
+    pl.semaphore_wait(barrier, expected)
+    m_f1 = exchange(f1, own_1, **wide)
+
     x4, y4, t4 = 2 * ngx, 2 * ngy, ngz
+    x5, y5, t5 = x4 // 2, y4 // 2, t4 // 2
+    x6, y6, t6 = x5 // 2, y5 // 2, t5 // 2
+    clear_outside(r1, own_1, **thin)
+    clear_outside(f2, own_2, **wide)
+    clear_outside(r2, own_2, **thin)
+    clear_outside(f3, own_3, **wide)
+    clear_outside(r3, own_3, **thin)
     for a in (f4, h4, r4, q4, k4):
         zero_faces(a, t4, x4, y4)
     c4[...] = jnp.zeros(c4.shape, F32)
     for a in (f5, h5, r5, q5, k5):
-        zero_faces(a, t4 // 2, x4 // 2, y4 // 2)
+        zero_faces(a, t5, x5, y5)
     for a in (f6, a6, b6):
-        zero_faces(a, t4 // 4, x4 // 4, y4 // 4)
+        zero_faces(a, t6, x6, y6)
     acc[...] = jnp.zeros(acc.shape, F32)
     acc4[...] = jnp.zeros(acc4.shape, F32)
 
-    for c in loads:
-        c.wait()
-    pl.semaphore_wait(barrier, expected)
+    inside = [tuple(c.astype(F32) for c in (p > 0, p < n - 1)) for p, n in zip(me, sizes)]
+
+    def row_mask(n, first, own):
+        row = lax.broadcasted_iota(jnp.int32, (n, LANES), 0)
+        one = jnp.ones((n, LANES), F32)
+        return jnp.where(row < first, one * inside[1][0], jnp.where(row >= first + own, one * inside[1][1], one))
+
+    def side(axis, i, own):
+        return inside[axis][0] if i < 0 else inside[axis][1] if i >= own else None
+
+    def masked(v, mask, *scalars):
+        v = v * mask
+        for s in scalars:
+            if s is not None:
+                v = v * s
+        return v
+
+    def first_step(h, f, own):
+        tiles, planes, rows = own
+        mask = row_mask(rows + 2, 1, rows)
+
+        def own_tile(t):
+            for x in range(-1, planes + 1):
+                v = smooth(f, t + 2, x + 2, YO - 1, rows + 2)
+                h[t + 1, x + 1, pl.ds(YO - 1, rows + 2), :] = masked(v, mask, side(0, x, planes))
+
+        loop(tiles, own_tile)
+        for t in (-1, tiles):
+            for x in range(planes):
+                h[t + 1, x + 1, pl.ds(YO, rows), :] = smooth(f, t + 2, x + 2, YO, rows) * side(2, t, tiles)
 
     def apply(dst, src, tiles, planes, rows):
         def body(t):
@@ -266,29 +295,33 @@
 
         loop(tiles, body)
 
-    def restrict(dst, r, tiles, planes, rows):
+    def restrict(dst, r, tiles, planes, rows, first=1):
         def body(tc):
             for xc in range(planes):
-                dst[tc + 1, xc + 1, pl.ds(YO, rows), :] = coarse_cell(r, tc, xc, rows)
+                dst[tc + first, xc + first, pl.ds(YO, rows), :] = coarse_cell(r, tc, xc, rows)
 
         loop(tiles, body)
 
-    def collect(w, f, h, r, tiles, planes, rows, x0, y0, level):
+    def collect(w, f, h, r, own, x0, y0, level):
+        tiles, planes, rows = own
+
         def body(t):
             for x in range(planes):
                 at = (t + 1, x + 1, pl.ds(YO, rows), slice(None))
-                v = f[at] + h[at] + r[at] + smooth(r, t + 1, x + 1, YO, rows)
+                v = f[t + 2, x + 2, pl.ds(YO, rows), :] + h[at] + r[at] + smooth(r, t + 1, x + 1, YO, rows)
                 w[t + (x0 > 0), x + x0, pl.ds(y0, rows), :] = v * tau(level)
 
         loop(tiles, body)
 
-    def energy(f, h, r, tiles, planes, rows, level):
+    def energy(f, h, r, own, level):
+        tiles, planes, rows = own
         padded = -(-rows // 8) * 8
         keep = lax.broadcasted_iota(jnp.int32, (1, padded, 1), 1) < rows
 
         def body(t):
+            vf = f[t + 2, pl.ds(2, planes), pl.ds(YO, padded), :]
             at = (t + 1, pl.ds(1, planes), pl.ds(YO, padded), slice(None))
-            vf, vh, vr = f[at], h[at], r[at]
+            vh, vr = h[at], r[at]
             if padded != rows:
                 vf, vh, vr = (jnp.where(keep, v, 0.0) for v in (vf, vh, vr))
             vf, vh, vr = (v.reshape(planes * padded, LANES) for v in (vf, vh, vr))
@@ -296,31 +329,22 @@
 
         loop(tiles, body)
 
-    wait(faces(f1, 8, 16, 16))
-    apply(h1, f1, 8, 16, 16)
-    wait(faces(h1, 8, 16, 16))
+    wait(m_f1)
+    first_step(h1, f1, own_1)
     apply(r1, h1, 8, 16, 16)
-    restrict(f2, r1, 4, 8, 8)
-    m_f2 = faces(f2, 4, 8, 8)
-    m_r1 = faces(r1, 8, 16, 16)
-    energy(f1, h1, r1, 8, 16, 16, 1)
+    restrict(f2, r1, 4, 8, 8, 2)
+    m_f2 = exchange(f2, own_2, **wide)
+    m_r1 = exchange(r1, own_1, **thin)
+    energy(f1, h1, r1, own_1, 1)
     wait(m_f2)
-    apply(h2, f2, 4, 8, 8)
-    m_h2 = faces(h2, 4, 8, 8)
-    wait(m_r1)
-    collect(w1, f1, h1, r1, 8, 16, 16, 0, 0, 1)
-    wait(m_h2)
+    first_step(h2, f2, own_2)
     apply(r2, h2, 4, 8, 8)
-    restrict(f3, r2, 2, 4, 4)
-    m_f3 = faces(f3, 2, 4, 4)
-    m_r2 = faces(r2, 4, 8, 8)
-    energy(f2, h2, r2, 4, 8, 8, 2)
+    restrict(f3, r2, 2, 4, 4, 2)
+    m_f3 = exchange(f3, own_3, **wide)
+    m_r2 = exchange(r2, own_2, **thin)
+    energy(f2, h2, r2, own_2, 2)
     wait(m_f3)
-    apply(h3, f3, 2, 4, 4)
-    m_h3 = faces(h3, 2, 4, 4)
-    wait(m_r2)
-    collect(w2, f2, h2, r2, 4, 8, 8, 1, 1, 2)
-    wait(m_h3)
+    first_step(h3, f3, own_3)
     apply(r3, h3, 2, 4, 4)
 
     own_x, own_y = pl.ds(2 * gx + 1, 2), pl.ds(YO + 2 * gy, 2)
@@ -331,12 +355,14 @@
     m_z = start(
         [Msg(block, block, {"gz": lax.rem(gz + d, ngz)}, None, None) for d in range(1, ngz)]
     )
-    m_r3 = faces(r3, 2, 4, 4)
-    m_w2 = rims(w2, 4, 8, 8, 1, False)
+    m_r3 = exchange(r3, own_3, **thin)
+    wait(m_r2)
+    collect(w2, f2, h2, r2, own_2, 1, 1, 2)
+    m_w2 = exchange(w2, own_2, first=(1, 1, 1), widths={1: 1, 2: 1})
     wait(m_r3)
-    energy(f3, h3, r3, 2, 4, 4, 3)
-    collect(w3, f3, h3, r3, 2, 4, 4, 2, 2, 3)
-    m_w3 = rims(w3, 2, 4, 4, 2, True)
+    collect(w3, f3, h3, r3, own_3, 2, 2, 3)
+    m_w3 = exchange(w3, own_3, first=(1, 2, 2), widths={1: 2, 2: 2, 3: 2})
+    energy(f3, h3, r3, own_3, 3)
     piece = 32 // ngz
     square = acc[0:PAIRS, :] + swap(acc[PAIRS:, :])
     packed = jnp.where(low_lanes(), square[0:32, :], swap(square[32:64, :]))
@@ -358,6 +384,8 @@
                 to = {"gx": lax.rem(chip + dx, chips) * 2 + core, "gy": lax.rem(gy + dy, ngy)}
                 m_p.append(Msg(line, line, to, None, None))
     start(m_p)
+    wait(m_r1)
+    collect(w1, f1, h1, r1, own_1, 0, 0, 1)
     wait(m_ca)
     total = ca[0]
     for k in range(1, ngz):
@@ -376,8 +404,6 @@
 
     apply(h4, f4, t4, x4, y4)
     apply(r4, h4, t4, x4, y4)
-    x5, y5, t5 = x4 // 2, y4 // 2, t4 // 2
-    x6, y6, t6 = x5 // 2, y5 // 2, t5 // 2
     restrict(f5, r4, t5, x5, y5)
     apply(h5, f5, t5, x5, y5)
     apply(r5, h5, t5, x5, y5)
@@ -434,25 +460,6 @@
         [Msg(ct, cc.at[gz], {"gz": lax.rem(gz + d, ngz)}, None, None) for d in range(1, ngz)]
     )
 
-    inside = [
-        tuple(c.astype(F32) for c in (p > 0, p < n - 1)) for p, n in zip(me, sizes)
-    ]
-
-    def row_mask(n, first, own):
-        row = lax.broadcasted_iota(jnp.int32, (n, LANES), 0)
-        one = jnp.ones((n, LANES), F32)
-        return jnp.where(row < first, one * inside[1][0], jnp.where(row >= first + own, one * inside[1][1], one))
-
-    def side(axis, i, own):
-        return inside[axis][0] if i < 0 else inside[axis][1] if i >= own else None
-
-    def masked(v, mask, *scalars):
-        v = v * mask
-        for s in scalars:
-            if s is not None:
-                v = v * s
-        return v
-
     wait(m_w3)
     for j in range(3):
         for i in range(6):
@@ -545,9 +552,10 @@
 
     t4, x4, y4 = ngz, 2 * ngx, 2 * ngy
     l1, l2, l3 = level(8, 16, 16), level(4, 8, 8), level(2, 4, 4)
+    e1, e2, e3 = field(12, 20, 32), field(8, 12, 24), field(6, 8, 16)
     l4, l5, l6 = (level(t4 // s, x4 // s, y4 // s) for s in (1, 2, 4))
     c4 = field(t4 + 2, x4 + 4, 24)
-    scratch = [l1, l1, l1, field(8, 16, 16), l2, l2, l2, field(6, 10, 16), l3, l3, l3, field(4, 8, 8)]
+    scratch = [e1, l1, l1, field(8, 16, 16), e2, l2, l2, field(6, 10, 16), e3, l3, l3, field(4, 8, 8)]
     scratch += [l4, l4, l4, l4, l4, c4, l5, l5, l5, l5, l5, l5, l6, l6, l6]
     scratch += [field(8, 12, 16), field(8, 12, 16), field(1, 1, 8), field(10, 16, 16), field(10, 16, 16), field(1, 1, 8)]
     scratch += [field(12, 20, 24), field(12, 20, 24), field(8, 16, 16)]
@@ -555,7 +563,7 @@
     row = pltpu.VMEM((piece, LANES), F32)
     scratch += [square, square, pltpu.VMEM((ngz, piece, LANES), F32), pltpu.VMEM((ngz, piece, LANES), F32), row]
     scratch += [pltpu.VMEM((ngx * ngy, piece, LANES), F32), row, pltpu.VMEM((ngz, piece, LANES), F32)]
-    messages = 54 + 18 + 26 + 3 * (ngz - 1) + (ngx // 2 * ngy - 1) + (ngx * ngy - 1) + ngx // 2
+    messages = 3 * (18 + 6) + 18 + 26 + 3 * (ngz - 1) + (ngx // 2 * ngy - 1) + (ngx * ngy - 1) + ngx // 2
     scratch += [pltpu.SemaphoreType.DMA((messages,)), pltpu.SemaphoreType.DMA((messages,)), pltpu.SemaphoreType.DMA((8,))]
     return pl.pallas_call(
         functools.partial(kernel, nums),

time: 72.8 us -> 63.5 us (0.87)
  Pallas kernels: 69.1 us -> 59.8 us
    pallas_call x1, Pallas kernels: 69.1 us -> 59.8 us  [local(): pl.pallas_call(functools.partial(kernel, nums), out_shape=(jax.ShapeDtype...]
where the time goes in v2:
time: 63.5 us; the launch traced here: 63.4 us
  Pallas kernels  59.8 us (94%)
  local copies, waits for them, and re-layouts  2.93 us (5%)
  between operations  0.65 us (1%)
    pallas_call x1, Pallas kernels, local(): pl.pallas_call(functools.partial(kernel, nums), out_shape=(jax.ShapeDtype...  59.8 us
    unnamed x4, local copies, waits for them, and re-layouts  2.93 us

profile of v2, /device:TPU:1, one launch (start us, length us, event | category | flops | bytes accessed | tf_op | source)
XLA Modules:
  0.0 63.4 jit_solution(6334011854987324361)
XLA Ops:
  0.6 59.8 %cycle.1 = (f32[16,16,1024]{2,1,0:T(8,128)}, f32[64,64]{1,0:T(8,128)}) custom-call(f32[16,16,1024]{2,1,0:T(8,128)} %dens.1), custom_call_target="tpu_custom_call" | custom-call | tf_op jit(solution)/shard_map/cycle/pallas_call | solution.py:568
  60.4 0.0 copy-start
  60.4 2.3 %copy.5 = f32[16,16,1024]{2,1,0:T(8,128)} copy(f32[16,16,1024]{2,1,0:T(8,128)} %get-tuple-element.4) | data formatting | bytes 2097152
  62.7 0.0 copy-done
  62.7 0.6 copy.6
Async XLA Ops:
  60.4 2.3 %copy-start = (f32[64,64]{1,0:T(8,128)S(1)}, f32[64,64]{1,0:T(8,128)}, u32[]{:S(2)}) copy-start(f32[64,64]{1,0:T(8,128)} %get-tuple-element.5) | copy-start | bytes 49156

commit v3 on v2

--- a/solution.py
+++ b/solution.py
@@ -85,7 +85,8 @@
     def dot(u, v):
         return lax.dot_general(u, v, (((0,), (0,)), ((), ())), preferred_element_type=F32)
 
-    return dot(ah, bh) + (dot(ah, bl) + dot(al, bh))
+    both = dot(ah, jnp.concatenate([bh, bl], axis=1))
+    return both[:, :LANES] + (both[:, LANES:] + dot(al, bh))
 
 
 def kernel(
@@ -313,21 +314,26 @@
 
         loop(tiles, body)
 
-    def energy(f, h, r, own, level):
+    def energy(a, b, own, level):
         tiles, planes, rows = own
         padded = -(-rows // 8) * 8
-        keep = lax.broadcasted_iota(jnp.int32, (1, padded, 1), 1) < rows
-
-        def body(t):
-            vf = f[t + 2, pl.ds(2, planes), pl.ds(YO, padded), :]
-            at = (t + 1, pl.ds(1, planes), pl.ds(YO, padded), slice(None))
-            vh, vr = h[at], r[at]
-            if padded != rows:
-                vf, vh, vr = (jnp.where(keep, v, 0.0) for v in (vf, vh, vr))
-            vf, vh, vr = (v.reshape(planes * padded, LANES) for v in (vf, vh, vr))
-            acc[...] += (dot_t(vf, vf + vh) + dot_t(vh, vh + vr)) * (tau(level) * 8.0 ** (level - 1))
-
-        loop(tiles, body)
+        step = min(tiles, 4)
+
+        def body(i):
+            both = []
+            for t in range(step):
+                v = a(i * step + t, rows), b(i * step + t, rows)
+                if padded != rows:
+                    none = jnp.zeros((planes, padded - rows, LANES), F32)
+                    v = tuple(jnp.concatenate([u, none], axis=1) for u in v)
+                both.append([u.reshape(planes * padded, LANES) for u in v])
+            va, vb = (jnp.concatenate(u, axis=0) for u in zip(*both))
+            acc[...] += dot_t(va, vb) * 8.0 ** (level - 1)
+
+        loop(tiles // step, body)
+
+    def cells(a, own, first):
+        return lambda t, n: a[t + first[0], pl.ds(first[1], own[1]), pl.ds(first[2], n), :]
 
     wait(m_f1)
     first_step(h1, f1, own_1)
@@ -335,14 +341,15 @@
     restrict(f2, r1, 4, 8, 8, 2)
     m_f2 = exchange(f2, own_2, **wide)
     m_r1 = exchange(r1, own_1, **thin)
-    energy(f1, h1, r1, own_1, 1)
+    in_f1, in_h1, in_r1 = (cells(a, own_1, (i, i, YO)) for a, i in ((f1, 2), (h1, 1), (r1, 1)))
+    energy(in_f1, lambda t, n: (in_f1(t, n) + in_h1(t, n)) * tau(1), own_1, 1)
     wait(m_f2)
     first_step(h2, f2, own_2)
     apply(r2, h2, 4, 8, 8)
     restrict(f3, r2, 2, 4, 4, 2)
     m_f3 = exchange(f3, own_3, **wide)
     m_r2 = exchange(r2, own_2, **thin)
-    energy(f2, h2, r2, own_2, 2)
+    energy(in_h1, lambda t, n: (in_h1(t, n) + in_r1(t, n)) * tau(1), own_1, 1)
     wait(m_f3)
     first_step(h3, f3, own_3)
     apply(r3, h3, 2, 4, 4)
@@ -358,11 +365,10 @@
     m_r3 = exchange(r3, own_3, **thin)
     wait(m_r2)
     collect(w2, f2, h2, r2, own_2, 1, 1, 2)
-    m_w2 = exchange(w2, own_2, first=(1, 1, 1), widths={1: 1, 2: 1})
+    energy(cells(f2, own_2, (2, 2, YO)), cells(w2, own_2, (1, 1, 1)), own_2, 2)
     wait(m_r3)
     collect(w3, f3, h3, r3, own_3, 2, 2, 3)
-    m_w3 = exchange(w3, own_3, first=(1, 2, 2), widths={1: 2, 2: 2, 3: 2})
-    energy(f3, h3, r3, own_3, 3)
+    energy(cells(f3, own_3, (2, 2, YO)), cells(w3, own_3, (1, 2, 2)), own_3, 3)
     piece = 32 // ngz
     square = acc[0:PAIRS, :] + swap(acc[PAIRS:, :])
     packed = jnp.where(low_lanes(), square[0:32, :], swap(square[32:64, :]))
@@ -384,6 +390,8 @@
                 to = {"gx": lax.rem(chip + dx, chips) * 2 + core, "gy": lax.rem(gy + dy, ngy)}
                 m_p.append(Msg(line, line, to, None, None))
     start(m_p)
+    m_w3 = exchange(w3, own_3, first=(1, 2, 2), widths={1: 2, 2: 2, 3: 2})
+    m_w2 = exchange(w2, own_2, first=(1, 1, 1), widths={1: 1, 2: 1})
     wait(m_r1)
     collect(w1, f1, h1, r1, own_1, 0, 0, 1)
     wait(m_ca)
@@ -507,26 +515,24 @@
 
     def last(t):
         for x in range(16):
-            out[t, x] = w1[t, x] + smooth(k1, t + 2, x + 2, 2, 16)
+            v = w1[t, x] + smooth(k1, t + 2, x + 2, 2, 16)
+            pot[x, :, pl.ds(pl.multiple_of(t * LANES, LANES), LANES)] = v
 
     loop(8, last)
-    stores = [
-        pltpu.make_async_copy(out.at[t], pot.at[:, :, pl.ds(t * LANES, LANES)], io.at[t]) for t in range(8)
-    ]
-    for c in stores:
-        c.start()
-
     padded = -(-y4 // 8) * 8
     keep = lax.broadcasted_iota(jnp.int32, (1, padded, 1), 1) < y4
 
-    def level_4(t):
-        vf = f4[t + 1, pl.ds(1, x4), pl.ds(YO, padded), :]
-        vc = c4[t + 1, pl.ds(2, x4), pl.ds(YO, padded), :]
-        if padded != y4:
-            vf, vc = (jnp.where(keep, v, 0.0) for v in (vf, vc))
-        acc4[...] += dot_t(vf.reshape(x4 * padded, LANES), vc.reshape(x4 * padded, LANES))
-
-    loop(t4, level_4)
+    def level_4(i):
+        vf, vc = [], []
+        for t in range(4 * i, 4 * i + 4):
+            f, c = f4[t + 1, pl.ds(1, x4), pl.ds(YO, padded), :], c4[t + 1, pl.ds(2, x4), pl.ds(YO, padded), :]
+            if padded != y4:
+                f, c = (jnp.where(keep, v, 0.0) for v in (f, c))
+            vf.append(f.reshape(x4 * padded, LANES))
+            vc.append(c.reshape(x4 * padded, LANES))
+        acc4[...] += dot_t(jnp.concatenate(vf, axis=0), jnp.concatenate(vc, axis=0))
+
+    loop(t4 // 4, level_4)
     coarse_part = (acc4[0:PAIRS, :] + swap(acc4[PAIRS:, :])) * 512.0
     wait(m_cc)
     packed = jnp.concatenate([cc[k] for k in range(ngz)], axis=0)
@@ -534,8 +540,6 @@
     coul[0:32, :] = ((packed + coarse_part[0:32, :]) * scale)[:, :PAIRS]
     coul[32:64, :] = ((swap(packed) + coarse_part[32:64, :]) * scale)[:, :PAIRS]
 
-    for c in stores:
-        c.wait()
     for m in sent:
         m.drain()
 
@@ -567,15 +571,12 @@
     scratch += [pltpu.SemaphoreType.DMA((messages,)), pltpu.SemaphoreType.DMA((messages,)), pltpu.SemaphoreType.DMA((8,))]
     return pl.pallas_call(
         functools.partial(kernel, nums),
-        out_shape=(
-            jax.ShapeDtypeStruct(density.shape, F32),
-            jax.ShapeDtypeStruct((PAIRS, PAIRS), F32),
-        ),
+        out_shape=(pltpu.VMEM(density.shape, F32), pltpu.VMEM((PAIRS, PAIRS), F32)),
         in_specs=[pl.BlockSpec(memory_space=pl.ANY)],
-        out_specs=(pl.BlockSpec(memory_space=pl.ANY), pl.BlockSpec(memory_space=pltpu.VMEM)),
+        out_specs=(pl.BlockSpec(memory_space=pltpu.VMEM), pl.BlockSpec(memory_space=pltpu.VMEM)),
         scratch_shapes=scratch,
         compiler_params=pltpu.CompilerParams(
-            collective_id=0, has_side_effects=True, vmem_limit_bytes=60_000_000
+            collective_id=0, has_side_effects=True, vmem_limit_bytes=65_400_000
         ),
         name="cycle",
     )(density)

time: 63.5 us -> 60.4 us (0.951)
  Pallas kernels: 59.8 us -> 58 us
  local copies, waits for them, and re-layouts: 2.93 us -> 1.59 us
    pallas_call x1, Pallas kernels: 59.8 us -> 58 us  [local(): pl.pallas_call(functools.partial(kernel, nums), out_shape=(pltpu.VMEM(den...]
    unnamed x4 -> x2, local copies, waits for them, and re-layouts: 2.93 us -> 1.59 us
where the time goes in v3:
time: 60.4 us; the launch traced here: 60.3 us
  Pallas kernels  58 us (96%)
  local copies, waits for them, and re-layouts  1.59 us (3%)
  between operations  0.64 us (1%)
    pallas_call x1, Pallas kernels, local(): pl.pallas_call(functools.partial(kernel, nums), out_shape=(pltpu.VMEM(den...  58 us
    unnamed x2, local copies, waits for them, and re-layouts  1.59 us

profile of v3, /device:TPU:1, one launch (start us, length us, event | category | flops | bytes accessed | tf_op | source)
XLA Modules:
  0.0 60.3 jit_solution(9296643694800291496)
XLA Ops:
  0.6 58.0 %cycle.1 = (f32[16,16,1024]{2,1,0:T(8,128)S(1)}, f32[64,64]{1,0:T(8,128)S(1)}) custom-call(f32[16,16,1024]{2,1,0:T(8,128)} %dens.1), custom_call_target="tpu_custom_call" | custom-call | tf_op jit(solution)/shard_map/cycle/pallas_call | solution.py:572
  58.7 1.0 %copy.5 = f32[16,16,1024]{2,1,0:T(8,128)} copy(f32[16,16,1024]{2,1,0:T(8,128)S(1)} %get-tuple-element.2) | data formatting | bytes 2097152
  59.7 0.6 %copy.6 = f32[64,64]{1,0:T(8,128)} copy(f32[64,64]{1,0:T(8,128)S(1)} %get-tuple-element.3) | data formatting | bytes 32768

commit v4 on v3

--- a/solution.py
+++ b/solution.py
@@ -37,12 +37,19 @@
     return own * CENTRE + total * SIDE
 
 
-def loop(n, body, unroll_below=3):
-    if n < unroll_below:
+def loop(n, body, unroll_below=3, step=1):
+    if n < unroll_below or n <= step:
         for i in range(n):
             body(i)
-    else:
-        lax.fori_loop(0, n, lambda i, c: (body(i), c)[1], 0)
+        return
+    step = step if n % step == 0 else 1
+
+    def turn(i, carry):
+        for j in range(step):
+            body(i * step + j)
+        return carry
+
+    lax.fori_loop(0, n // step, turn, 0)
 
 
 def restrict_rows(r, t, x, rows):
@@ -92,7 +99,7 @@
 def kernel(
     nums, dens, pot, coul,
     f1, h1, r1, w1, f2, h2, r2, w2, f3, h3, r3, w3,
-    f4, h4, r4, q4, k4, c4, f5, h5, r5, q5, k5, c5, f6, a6, b6,
+    f4, h4, r4, q4, k4, c4, f5, h5, r5, q5, k5, c5, f6, d6, a6, b6,
     q3, k3, c3, q2, k2, c2, q1, k1, out,
     acc, acc4, cp, ca, cs, cb, ct, cc,
     send, recv, io,
@@ -146,11 +153,16 @@
 
         def drain(self):
             when(self.cond_send, self.copy.wait_send)
+            sent.remove(self)
 
     def start(msgs):
         for m in msgs:
             m.start()
         return msgs
+
+    def drain(msgs):
+        for m in msgs:
+            m.drain()
 
     def wait(msgs):
         for m in msgs:
@@ -211,8 +223,6 @@
     ]
     for c in loads:
         c.start()
-    w2[...] = jnp.zeros(w2.shape, F32)
-    w3[...] = jnp.zeros(w3.shape, F32)
     barrier = pltpu.get_barrier_semaphore()
     expected = jnp.int32(0)
     for o in offsets:
@@ -234,7 +244,6 @@
         pl.semaphore_signal(barrier, inc=1, device_id=other(dx, dy), device_id_type=MESH)
     expected = expected + (ngz - 1 + len(others))
 
-    clear_outside(f1, own_1, **wide)
     for c in loads:
         c.wait()
     pl.semaphore_wait(barrier, expected)
@@ -243,7 +252,12 @@
     x4, y4, t4 = 2 * ngx, 2 * ngy, ngz
     x5, y5, t5 = x4 // 2, y4 // 2, t4 // 2
     x6, y6, t6 = x5 // 2, y5 // 2, t5 // 2
+    rim_2 = dict(first=(1, 1, 1), widths={1: 1, 2: 1})
+    rim_3 = dict(first=(1, 2, 2), widths={1: 2, 2: 2, 3: 2})
+    clear_outside(f1, own_1, **wide)
     clear_outside(r1, own_1, **thin)
+    clear_outside(w2, own_2, **rim_2)
+    clear_outside(w3, own_3, **rim_3)
     clear_outside(f2, own_2, **wide)
     clear_outside(r2, own_2, **thin)
     clear_outside(f3, own_3, **wide)
@@ -253,8 +267,8 @@
     c4[...] = jnp.zeros(c4.shape, F32)
     for a in (f5, h5, r5, q5, k5):
         zero_faces(a, t5, x5, y5)
-    for a in (f6, a6, b6):
-        zero_faces(a, t6, x6, y6)
+    for a in (a6, b6):
+        zero_faces(a, 2 * t6, x6, y6)
     acc[...] = jnp.zeros(acc.shape, F32)
     acc4[...] = jnp.zeros(acc4.shape, F32)
 
@@ -264,6 +278,9 @@
         row = lax.broadcasted_iota(jnp.int32, (n, LANES), 0)
         one = jnp.ones((n, LANES), F32)
         return jnp.where(row < first, one * inside[1][0], jnp.where(row >= first + own, one * inside[1][1], one))
+
+    def tile_side(t, own):
+        return jnp.where(t < 0, inside[2][0], jnp.where(t >= own, inside[2][1], 1.0))
 
     def side(axis, i, own):
         return inside[axis][0] if i < 0 else inside[axis][1] if i >= own else None
@@ -284,7 +301,7 @@
                 v = smooth(f, t + 2, x + 2, YO - 1, rows + 2)
                 h[t + 1, x + 1, pl.ds(YO - 1, rows + 2), :] = masked(v, mask, side(0, x, planes))
 
-        loop(tiles, own_tile)
+        loop(tiles, own_tile, step=2 if planes <= 8 else 1)
         for t in (-1, tiles):
             for x in range(planes):
                 h[t + 1, x + 1, pl.ds(YO, rows), :] = smooth(f, t + 2, x + 2, YO, rows) * side(2, t, tiles)
@@ -294,14 +311,14 @@
             for x in range(1, planes + 1):
                 dst[t + 1, x, pl.ds(YO, rows), :] = smooth(src, t + 1, x, YO, rows)
 
-        loop(tiles, body)
+        loop(tiles, body, step=4 if planes <= 8 else 2 if rows <= 8 else 1)
 
     def restrict(dst, r, tiles, planes, rows, first=1):
         def body(tc):
             for xc in range(planes):
                 dst[tc + first, xc + first, pl.ds(YO, rows), :] = coarse_cell(r, tc, xc, rows)
 
-        loop(tiles, body)
+        loop(tiles, body, step=2)
 
     def collect(w, f, h, r, own, x0, y0, level):
         tiles, planes, rows = own
@@ -314,7 +331,7 @@
 
         loop(tiles, body)
 
-    def energy(a, b, own, level):
+    def energy(a, b, own, level, total=acc):
         tiles, planes, rows = own
         padded = -(-rows // 8) * 8
         step = min(tiles, 4)
@@ -328,9 +345,9 @@
                     v = tuple(jnp.concatenate([u, none], axis=1) for u in v)
                 both.append([u.reshape(planes * padded, LANES) for u in v])
             va, vb = (jnp.concatenate(u, axis=0) for u in zip(*both))
-            acc[...] += dot_t(va, vb) * 8.0 ** (level - 1)
-
-        loop(tiles // step, body)
+            total[...] += dot_t(va, vb) * 8.0 ** (level - 1)
+
+        loop(tiles // step, body, 2)
 
     def cells(a, own, first):
         return lambda t, n: a[t + first[0], pl.ds(first[1], own[1]), pl.ds(first[2], n), :]
@@ -350,6 +367,10 @@
     m_f3 = exchange(f3, own_3, **wide)
     m_r2 = exchange(r2, own_2, **thin)
     energy(in_h1, lambda t, n: (in_h1(t, n) + in_r1(t, n)) * tau(1), own_1, 1)
+    in_f2, in_h2, in_r2 = (cells(a, own_2, (i, i, YO)) for a, i in ((f2, 2), (h2, 1), (r2, 1)))
+    energy(in_f2, lambda t, n: (in_f2(t, n) + in_h2(t, n)) * tau(2), own_2, 2)
+    energy(in_h2, lambda t, n: (in_h2(t, n) + in_r2(t, n)) * tau(2), own_2, 2)
+    drain(m_f1)
     wait(m_f3)
     first_step(h3, f3, own_3)
     apply(r3, h3, 2, 4, 4)
@@ -363,12 +384,9 @@
         [Msg(block, block, {"gz": lax.rem(gz + d, ngz)}, None, None) for d in range(1, ngz)]
     )
     m_r3 = exchange(r3, own_3, **thin)
-    wait(m_r2)
-    collect(w2, f2, h2, r2, own_2, 1, 1, 2)
-    energy(cells(f2, own_2, (2, 2, YO)), cells(w2, own_2, (1, 1, 1)), own_2, 2)
-    wait(m_r3)
-    collect(w3, f3, h3, r3, own_3, 2, 2, 3)
-    energy(cells(f3, own_3, (2, 2, YO)), cells(w3, own_3, (1, 2, 2)), own_3, 3)
+    in_f3, in_h3, in_r3 = (cells(a, own_3, (i, i, YO)) for a, i in ((f3, 2), (h3, 1), (r3, 1)))
+    energy(in_f3, lambda t, n: (in_f3(t, n) + in_h3(t, n)) * tau(3), own_3, 3)
+    energy(in_h3, lambda t, n: (in_h3(t, n) + in_r3(t, n)) * tau(3), own_3, 3)
     piece = 32 // ngz
     square = acc[0:PAIRS, :] + swap(acc[PAIRS:, :])
     packed = jnp.where(low_lanes(), square[0:32, :], swap(square[32:64, :]))
@@ -380,7 +398,12 @@
         m_ca.append(Msg(cp.at[to], ca.at[gz], {"gz": to}, None, None))
     start(m_ca)
     ca[gz] = cp[gz]
-
+    wait(m_r2)
+    collect(w2, f2, h2, r2, own_2, 1, 1, 2)
+    wait(m_r3)
+    collect(w3, f3, h3, r3, own_3, 2, 2, 3)
+
+    drain(m_f2)
     wait(m_z)
     line = f4.at[all_t, own_x, own_y]
     m_p = []
@@ -390,10 +413,8 @@
                 to = {"gx": lax.rem(chip + dx, chips) * 2 + core, "gy": lax.rem(gy + dy, ngy)}
                 m_p.append(Msg(line, line, to, None, None))
     start(m_p)
-    m_w3 = exchange(w3, own_3, first=(1, 2, 2), widths={1: 2, 2: 2, 3: 2})
-    m_w2 = exchange(w2, own_2, first=(1, 1, 1), widths={1: 1, 2: 1})
-    wait(m_r1)
-    collect(w1, f1, h1, r1, own_1, 0, 0, 1)
+    m_w3 = exchange(w3, own_3, **rim_3)
+    m_w2 = exchange(w2, own_2, **rim_2)
     wait(m_ca)
     total = ca[0]
     for k in range(1, ngz):
@@ -402,6 +423,10 @@
     slot = gx * ngy + gy
     cb[slot] = total
     m_cb = start([Msg(cs, cb.at[slot], other(dx, dy), None, None) for dx, dy in others])
+    wait(m_r1)
+    collect(w1, f1, h1, r1, own_1, 0, 0, 1)
+    for m in (m_r1, m_f3, m_r2, m_r3, m_z, m_ca):
+        drain(m)
     wait(m_p)
     m_c = []
     for j in range(chips):
@@ -411,53 +436,6 @@
     wait(m_c)
 
     apply(h4, f4, t4, x4, y4)
-    apply(r4, h4, t4, x4, y4)
-    restrict(f5, r4, t5, x5, y5)
-    apply(h5, f5, t5, x5, y5)
-    apply(r5, h5, t5, x5, y5)
-    restrict(f6, r5, t6, x6, y6)
-    for t in range(1, t6 + 1):
-        for x in range(1, x6 + 1):
-            at = (t, x, pl.ds(YO, y6), slice(None))
-            v = f6[at] * tau(6)
-            f6[at] = v
-            a6[at] = v
-    now, later = a6, b6
-    for _ in range(7):
-        for t in range(1, t6 + 1):
-            for x in range(1, x6 + 1):
-                at = (t, x, pl.ds(YO, y6), slice(None))
-                later[at] = f6[at] + smooth(now, t, x, YO, y6)
-        now, later = later, now
-
-    def prolong(dst, value, tile, x, row, rows, which=(0, 1)):
-        turned = swap(value)
-        halves = (jnp.where(low_lanes(), value, turned), jnp.where(low_lanes(), turned, value))
-        for k in which:
-            for i in range(2):
-                for j in range(2):
-                    dst[tile + k, x + i, pl.ds(row + j, rows, stride=2), :] = halves[k]
-
-    def coarse_up(c, f, h, r, q, k, coarse, first, tiles, planes, rows, level, pad):
-        def spread(t):
-            for x in range(planes // 2):
-                value = coarse[t + 1, x + first, pl.ds(YO, rows // 2), :]
-                prolong(q, value, 2 * t + 1, 2 * x + 1, YO, rows // 2)
-
-        loop(tiles // 2, spread)
-        apply(k, q, tiles, planes, rows)
-
-        def body(t):
-            for x in range(1, planes + 1):
-                at = (t + 1, x, pl.ds(YO, rows), slice(None))
-                v = (f[at] + h[at] + r[at] + smooth(r, t + 1, x, YO, rows)) * tau(level)
-                c[t + 1, x + pad, pl.ds(YO, rows), :] = v + smooth(k, t + 1, x, YO, rows)
-
-        loop(tiles, body)
-
-    coarse_up(c5, f5, h5, r5, q5, k5, now, 1, t5, x5, y5, 5, 0)
-    coarse_up(c4, f4, h4, r4, q4, k4, c5, 1, t4, x4, y4, 4, 1)
-
     wait(m_cb)
     total = cb[0]
     for k in range(1, ngx * ngy):
@@ -468,49 +446,135 @@
         [Msg(ct, cc.at[gz], {"gz": lax.rem(gz + d, ngz)}, None, None) for d in range(1, ngz)]
     )
 
+    apply(r4, h4, t4, x4, y4)
+    restrict(f5, r4, t5, x5, y5)
+    apply(h5, f5, t5, x5, y5)
+    apply(r5, h5, t5, x5, y5)
+    restrict(f6, r5, t6, x6, y6)
+    cells_6 = [(z, x) for z in range(1, 2 * t6 + 1) for x in range(1, x6 + 1)]
+    for t in range(t6):
+        for x in range(1, x6 + 1):
+            v = f6[t + 1, x, pl.ds(YO, y6), :] * tau(6)
+            turned = swap(v)
+            for k, u in enumerate((jnp.where(low_lanes(), v, turned), jnp.where(low_lanes(), turned, v))):
+                d6[2 * t + 1 + k, x, pl.ds(YO, y6), :] = u
+                a6[2 * t + 1 + k, x, pl.ds(YO, y6), :] = u
+    now, later = a6, b6
+    for _ in range(7):
+        for z, x in cells_6:
+            own = pl.ds(YO, y6)
+            total = now[z, x, pl.ds(YO - 1, y6), :] + now[z, x, pl.ds(YO + 1, y6), :]
+            total = total + (now[z, x - 1, own, :] + now[z, x + 1, own, :])
+            total = total + (now[z - 1, x, own, :] + now[z + 1, x, own, :])
+            later[z, x, own, :] = d6[z, x, own, :] + (now[z, x, own, :] * CENTRE + total * SIDE)
+        now, later = later, now
+
+    def prolong(dst, value, tile, x, row, rows, which=(0, 1)):
+        turned = swap(value)
+        halves = (jnp.where(low_lanes(), value, turned), jnp.where(low_lanes(), turned, value))
+        for k in which:
+            for i in range(2):
+                for j in range(2):
+                    dst[tile + k, x + i, pl.ds(row + j, rows, stride=2), :] = halves[k]
+
+    def spread(q, coarse, tiles, planes, rows):
+        def body(t):
+            for x in range(planes):
+                prolong(q, coarse[t + 1, x + 1, pl.ds(YO, rows), :], 2 * t + 1, 2 * x + 1, YO, rows)
+
+        loop(tiles, body, step=2)
+
+    def solved(f, h, r, k, t, x, rows, level):
+        at = (t, x, pl.ds(YO, rows), slice(None))
+        return (f[at] + h[at] + r[at] + smooth(r, t, x, YO, rows)) * tau(level) + smooth(k, t, x, YO, rows)
+
+    for z, x in cells_6:
+        value = now[z, x, pl.ds(YO, y6), :]
+        for i in range(2):
+            for j in range(2):
+                q5[z, 2 * x - 1 + i, pl.ds(YO + j, y6, stride=2), :] = value
+    apply(k5, q5, t5, x5, y5)
+
+    def up_c5(t):
+        for x in range(1, x5 + 1):
+            c5[t + 1, x, pl.ds(YO, y5), :] = solved(f5, h5, r5, k5, t + 1, x, y5, 5)
+
+    loop(t5, up_c5, step=2)
+    spread(q4, c5, t5, x5, y5)
+
+    def up_k4(i):
+        t = jnp.clip(gz - 2 + i, 0, t4 - 1) + 1
+        for j in range(8):
+            x = jnp.clip(2 * gx - 3 + j, 0, x4 - 1) + 1
+            k4[t, x, pl.ds(YO, y4), :] = smooth(q4, t, x, YO, y4)
+
+    def up_c4(i):
+        t = jnp.clip(gz - 1 + i, 0, t4 - 1) + 1
+        for j in range(6):
+            x = jnp.clip(2 * gx - 2 + j, 0, x4 - 1) + 1
+            c4[t, x + 1, pl.ds(YO, y4), :] = solved(f4, h4, r4, k4, t, x, y4, 4)
+
+    loop(5, up_k4, step=5)
+    loop(3, up_c4, step=3)
+
     wait(m_w3)
-    for j in range(3):
+
+    def spread_3(j):
         for i in range(6):
             value = c4[gz + j, 2 * gx + i, pl.ds(YO - 2 + 2 * gy, 6), :]
             prolong(q3, value, 1 + 2 * j, 2 * i, 0, 6)
-    mask = row_mask(10, 3, 4)
-    for t in range(-2, 4):
+
+    loop(3, spread_3)
+    mask_k3, mask_c3 = row_mask(10, 3, 4), row_mask(8, 2, 4)
+
+    def up_k3(i):
+        mask = mask_k3 * tile_side(i - 2, 2)
         for x in range(-3, 7):
-            v = smooth(q3, t + 3, x + 4, 1, 10)
-            k3[t + 3, x + 4, pl.ds(1, 10), :] = masked(v, mask, side(2, t, 2), side(0, x, 4))
-    mask = row_mask(8, 2, 4)
-    for t in range(-1, 3):
+            v = smooth(q3, i + 1, x + 4, 1, 10)
+            k3[i + 1, x + 4, pl.ds(1, 10), :] = masked(v, mask, side(0, x, 4))
+
+    loop(6, up_k3, step=2)
+
+    def up_c3(i):
+        mask = mask_c3 * tile_side(i - 1, 2)
         for x in range(-2, 6):
-            v = w3[t + 1, x + 2, pl.ds(0, 8), :] + smooth(k3, t + 3, x + 4, 2, 8)
-            prolong(q2, masked(v, mask, side(2, t, 2), side(0, x, 4)), 2 * t + 3, 2 * x + 4, 0, 8)
+            v = w3[i, x + 2, pl.ds(0, 8), :] + smooth(k3, i + 2, x + 4, 2, 8)
+            prolong(q2, masked(v, mask, side(0, x, 4)), 2 * i + 1, 2 * x + 4, 0, 8)
+
+    loop(4, up_c3, step=2)
 
     wait(m_w2)
-    mask = row_mask(12, 2, 8)
-    for t in range(-1, 5):
+    mask_k2, mask_c2 = row_mask(12, 2, 8), row_mask(10, 1, 8)
+
+    def up_k2(i):
+        mask = mask_k2 * tile_side(i - 1, 4)
         for x in range(-2, 10):
-            v = smooth(q2, t + 3, x + 4, 2, 12)
-            k2[t + 3, x + 4, pl.ds(2, 12), :] = masked(v, mask, side(2, t, 4), side(0, x, 8))
-    mask = row_mask(10, 1, 8)
-    for t in range(-1, 5):
+            v = smooth(q2, i + 2, x + 4, 2, 12)
+            k2[i + 2, x + 4, pl.ds(2, 12), :] = masked(v, mask, side(0, x, 8))
+
+    loop(6, up_k2, step=2)
+
+    def up_c2(i):
+        mask = mask_c2 * tile_side(i - 1, 4)
         for x in range(-1, 9):
-            v = w2[t + 1, x + 1, pl.ds(0, 10), :] + smooth(k2, t + 3, x + 4, 3, 10)
-            which = (1,) if t < 0 else (0,) if t >= 4 else (0, 1)
-            prolong(q1, masked(v, mask, side(2, t, 4), side(0, x, 8)), 2 * t + 2, 2 * x + 2, 0, 10, which)
+            v = w2[i, x + 1, pl.ds(0, 10), :] + smooth(k2, i + 2, x + 4, 3, 10)
+            prolong(q1, masked(v, mask, side(0, x, 8)), 2 * i, 2 * x + 2, 0, 10)
+
+    loop(6, up_c2, step=2)
 
     mask = row_mask(18, 1, 16)
-
-    def rim_tile(t):
-        for x in range(0, 16):
-            v = smooth(q1, t + 2, x + 2, 1, 18)
-            k1[t + 2, x + 2, pl.ds(1, 18), :] = masked(v, mask, side(2, t, 8))
 
     def own_tile(t):
         for x in range(-1, 17):
             v = smooth(q1, t + 2, x + 2, 1, 18)
             k1[t + 2, x + 2, pl.ds(1, 18), :] = masked(v, mask, side(0, x, 16))
 
-    rim_tile(-1)
-    rim_tile(8)
+    def rim_tile(i):
+        for x in range(16):
+            v = smooth(q1, 9 * i + 1, x + 2, 2, 16)
+            k1[9 * i + 1, x + 2, pl.ds(2, 16), :] = v * jnp.where(i > 0, inside[2][1], inside[2][0])
+
+    loop(2, rim_tile, 2)
     loop(8, own_tile)
 
     def last(t):
@@ -519,29 +583,19 @@
             pot[x, :, pl.ds(pl.multiple_of(t * LANES, LANES), LANES)] = v
 
     loop(8, last)
-    padded = -(-y4 // 8) * 8
-    keep = lax.broadcasted_iota(jnp.int32, (1, padded, 1), 1) < y4
-
-    def level_4(i):
-        vf, vc = [], []
-        for t in range(4 * i, 4 * i + 4):
-            f, c = f4[t + 1, pl.ds(1, x4), pl.ds(YO, padded), :], c4[t + 1, pl.ds(2, x4), pl.ds(YO, padded), :]
-            if padded != y4:
-                f, c = (jnp.where(keep, v, 0.0) for v in (f, c))
-            vf.append(f.reshape(x4 * padded, LANES))
-            vc.append(c.reshape(x4 * padded, LANES))
-        acc4[...] += dot_t(jnp.concatenate(vf, axis=0), jnp.concatenate(vc, axis=0))
-
-    loop(t4 // 4, level_4)
-    coarse_part = (acc4[0:PAIRS, :] + swap(acc4[PAIRS:, :])) * 512.0
+    in_f4, in_h4, in_r4 = (cells(a, (t4, x4, y4), (1, 1, YO)) for a in (f4, h4, r4))
+    energy(in_f4, lambda t, n: (in_f4(t, n) + in_h4(t, n)) * tau(4), (t4, x4, y4), 4, acc4)
+    energy(in_h4, lambda t, n: (in_h4(t, n) + in_r4(t, n)) * tau(4), (t4, x4, y4), 4, acc4)
+    in_f5, in_c5 = (cells(a, (t5, x5, y5), (1, 1, YO)) for a in (f5, c5))
+    energy(in_f5, in_c5, (t5, x5, y5), 5, acc4)
+    coarse_part = acc4[0:PAIRS, :] + swap(acc4[PAIRS:, :])
     wait(m_cc)
     packed = jnp.concatenate([cc[k] for k in range(ngz)], axis=0)
     scale = 4.0 / (ngx * ngy * ngz * 16 * 16 * 16)
     coul[0:32, :] = ((packed + coarse_part[0:32, :]) * scale)[:, :PAIRS]
     coul[32:64, :] = ((swap(packed) + coarse_part[32:64, :]) * scale)[:, :PAIRS]
 
-    for m in sent:
-        m.drain()
+    drain(tuple(sent))
 
 
 def local(nums, density):
@@ -558,9 +612,10 @@
     l1, l2, l3 = level(8, 16, 16), level(4, 8, 8), level(2, 4, 4)
     e1, e2, e3 = field(12, 20, 32), field(8, 12, 24), field(6, 8, 16)
     l4, l5, l6 = (level(t4 // s, x4 // s, y4 // s) for s in (1, 2, 4))
+    e6 = level(t4 // 2, x4 // 4, y4 // 4)
     c4 = field(t4 + 2, x4 + 4, 24)
     scratch = [e1, l1, l1, field(8, 16, 16), e2, l2, l2, field(6, 10, 16), e3, l3, l3, field(4, 8, 8)]
-    scratch += [l4, l4, l4, l4, l4, c4, l5, l5, l5, l5, l5, l5, l6, l6, l6]
+    scratch += [l4, l4, l4, l4, l4, c4, l5, l5, l5, l5, l5, l5, l6, e6, e6, e6]
     scratch += [field(8, 12, 16), field(8, 12, 16), field(1, 1, 8), field(10, 16, 16), field(10, 16, 16), field(1, 1, 8)]
     scratch += [field(12, 20, 24), field(12, 20, 24), field(8, 16, 16)]
     square = pltpu.VMEM((LANES, LANES), F32)

time: 60.4 us -> 54.9 us (0.909)
  Pallas kernels: 58 us -> 52.6 us
    pallas_call x1, Pallas kernels: 58 us -> 52.6 us  [local(): pl.pallas_call(functools.partial(kernel, nums), out_shape=(pltpu.VMEM(den...]
where the time goes in v4:
time: 54.9 us; the launch traced here: 54.8 us
  Pallas kernels  52.6 us (96%)
  local copies, waits for them, and re-layouts  1.59 us (3%)
  between operations  0.64 us (1%)
    pallas_call x1, Pallas kernels, local(): pl.pallas_call(functools.partial(kernel, nums), out_shape=(pltpu.VMEM(den...  52.6 us
    unnamed x2, local copies, waits for them, and re-layouts  1.59 us

profile of v4, /device:TPU:1, one launch (start us, length us, event | category | flops | bytes accessed | tf_op | source)
XLA Modules:
  0.0 54.8 jit_solution(5750134626424524000)
XLA Ops:
  0.6 52.6 %cycle.1 = (f32[16,16,1024]{2,1,0:T(8,128)S(1)}, f32[64,64]{1,0:T(8,128)S(1)}) custom-call(f32[16,16,1024]{2,1,0:T(8,128)} %dens.1), custom_call_target="tpu_custom_call" | custom-call | tf_op jit(solution)/shard_map/cycle/pallas_call | solution.py:627
  53.2 1.0 %copy.5 = f32[16,16,1024]{2,1,0:T(8,128)} copy(f32[16,16,1024]{2,1,0:T(8,128)S(1)} %get-tuple-element.2) | data formatting | bytes 2097152
  54.2 0.6 %copy.6 = f32[64,64]{1,0:T(8,128)} copy(f32[64,64]{1,0:T(8,128)S(1)} %get-tuple-element.3) | data formatting | bytes 32768

commit v5 on v4

--- a/solution.py
+++ b/solution.py
@@ -301,7 +301,7 @@
                 v = smooth(f, t + 2, x + 2, YO - 1, rows + 2)
                 h[t + 1, x + 1, pl.ds(YO - 1, rows + 2), :] = masked(v, mask, side(0, x, planes))
 
-        loop(tiles, own_tile, step=2 if planes <= 8 else 1)
+        loop(tiles, own_tile, step=2)
         for t in (-1, tiles):
             for x in range(planes):
                 h[t + 1, x + 1, pl.ds(YO, rows), :] = smooth(f, t + 2, x + 2, YO, rows) * side(2, t, tiles)
@@ -311,7 +311,7 @@
             for x in range(1, planes + 1):
                 dst[t + 1, x, pl.ds(YO, rows), :] = smooth(src, t + 1, x, YO, rows)
 
-        loop(tiles, body, step=4 if planes <= 8 else 2 if rows <= 8 else 1)
+        loop(tiles, body, step=4 if planes <= 8 else 2)
 
     def restrict(dst, r, tiles, planes, rows, first=1):
         def body(tc):
@@ -499,7 +499,7 @@
         for x in range(1, x5 + 1):
             c5[t + 1, x, pl.ds(YO, y5), :] = solved(f5, h5, r5, k5, t + 1, x, y5, 5)
 
-    loop(t5, up_c5, step=2)
+    loop(t5, up_c5, step=4)
     spread(q4, c5, t5, x5, y5)
 
     def up_k4(i):
@@ -524,7 +524,7 @@
             value = c4[gz + j, 2 * gx + i, pl.ds(YO - 2 + 2 * gy, 6), :]
             prolong(q3, value, 1 + 2 * j, 2 * i, 0, 6)
 
-    loop(3, spread_3)
+    loop(3, spread_3, step=3)
     mask_k3, mask_c3 = row_mask(10, 3, 4), row_mask(8, 2, 4)
 
     def up_k3(i):
@@ -533,7 +533,7 @@
             v = smooth(q3, i + 1, x + 4, 1, 10)
             k3[i + 1, x + 4, pl.ds(1, 10), :] = masked(v, mask, side(0, x, 4))
 
-    loop(6, up_k3, step=2)
+    loop(6, up_k3, step=6)
 
     def up_c3(i):
         mask = mask_c3 * tile_side(i - 1, 2)
@@ -541,7 +541,7 @@
             v = w3[i, x + 2, pl.ds(0, 8), :] + smooth(k3, i + 2, x + 4, 2, 8)
             prolong(q2, masked(v, mask, side(0, x, 4)), 2 * i + 1, 2 * x + 4, 0, 8)
 
-    loop(4, up_c3, step=2)
+    loop(4, up_c3, step=4)
 
     wait(m_w2)
     mask_k2, mask_c2 = row_mask(12, 2, 8), row_mask(10, 1, 8)
@@ -552,7 +552,7 @@
             v = smooth(q2, i + 2, x + 4, 2, 12)
             k2[i + 2, x + 4, pl.ds(2, 12), :] = masked(v, mask, side(0, x, 8))
 
-    loop(6, up_k2, step=2)
+    loop(6, up_k2, step=3)
 
     def up_c2(i):
         mask = mask_c2 * tile_side(i - 1, 4)
@@ -560,7 +560,7 @@
             v = w2[i, x + 1, pl.ds(0, 10), :] + smooth(k2, i + 2, x + 4, 3, 10)
             prolong(q1, masked(v, mask, side(0, x, 8)), 2 * i, 2 * x + 2, 0, 10)
 
-    loop(6, up_c2, step=2)
+    loop(6, up_c2, step=3)
 
     mask = row_mask(18, 1, 16)
 
@@ -575,14 +575,14 @@
             k1[9 * i + 1, x + 2, pl.ds(2, 16), :] = v * jnp.where(i > 0, inside[2][1], inside[2][0])
 
     loop(2, rim_tile, 2)
-    loop(8, own_tile)
+    loop(8, own_tile, step=2)
 
     def last(t):
         for x in range(16):
             v = w1[t, x] + smooth(k1, t + 2, x + 2, 2, 16)
             pot[x, :, pl.ds(pl.multiple_of(t * LANES, LANES), LANES)] = v
 
-    loop(8, last)
+    loop(8, last, step=2)
     in_f4, in_h4, in_r4 = (cells(a, (t4, x4, y4), (1, 1, YO)) for a in (f4, h4, r4))
     energy(in_f4, lambda t, n: (in_f4(t, n) + in_h4(t, n)) * tau(4), (t4, x4, y4), 4, acc4)
     energy(in_h4, lambda t, n: (in_h4(t, n) + in_r4(t, n)) * tau(4), (t4, x4, y4), 4, acc4)

time: 54.9 us -> 53 us (0.965)
  Pallas kernels: 52.6 us -> 50.6 us
    pallas_call x1, Pallas kernels: 52.6 us -> 50.6 us  [local(): pl.pallas_call(functools.partial(kernel, nums), out_shape=(pltpu.VMEM(den...]
where the time goes in v5:
time: 53 us; the launch traced here: 52.9 us
  Pallas kernels  50.6 us (95%)
  local copies, waits for them, and re-layouts  1.59 us (3%)
  between operations  0.64 us (1%)
    pallas_call x1, Pallas kernels, local(): pl.pallas_call(functools.partial(kernel, nums), out_shape=(pltpu.VMEM(den...  50.6 us
    unnamed x2, local copies, waits for them, and re-layouts  1.59 us

profile of v5, /device:TPU:1, one launch (start us, length us, event | category | flops | bytes accessed | tf_op | source)
XLA Modules:
  0.0 52.9 jit_solution(9334335680657326774)
XLA Ops:
  0.6 50.6 %cycle.1 = (f32[16,16,1024]{2,1,0:T(8,128)S(1)}, f32[64,64]{1,0:T(8,128)S(1)}) custom-call(f32[16,16,1024]{2,1,0:T(8,128)} %dens.1), custom_call_target="tpu_custom_call" | custom-call | tf_op jit(solution)/shard_map/cycle/pallas_call | solution.py:627
  51.3 1.0 %copy.5 = f32[16,16,1024]{2,1,0:T(8,128)} copy(f32[16,16,1024]{2,1,0:T(8,128)S(1)} %get-tuple-element.2) | data formatting | bytes 2097152
  52.2 0.6 %copy.6 = f32[64,64]{1,0:T(8,128)} copy(f32[64,64]{1,0:T(8,128)S(1)} %get-tuple-element.3) | data formatting | bytes 32768

commit v6 on v5

--- a/solution.py
+++ b/solution.py
@@ -311,14 +311,14 @@
             for x in range(1, planes + 1):
                 dst[t + 1, x, pl.ds(YO, rows), :] = smooth(src, t + 1, x, YO, rows)
 
-        loop(tiles, body, step=4 if planes <= 8 else 2)
+        loop(tiles, body, step=4 if rows <= 8 else 2)
 
     def restrict(dst, r, tiles, planes, rows, first=1):
         def body(tc):
             for xc in range(planes):
                 dst[tc + first, xc + first, pl.ds(YO, rows), :] = coarse_cell(r, tc, xc, rows)
 
-        loop(tiles, body, step=2)
+        loop(tiles, body, step=4)
 
     def collect(w, f, h, r, own, x0, y0, level):
         tiles, planes, rows = own

time: 53 us -> 52.5 us (level)
  no operation moved by 1% of the time
where the time goes in v6:
time: 52.5 us; the launch traced here: 52.4 us
  Pallas kernels  50.2 us (96%)
  local copies, waits for them, and re-layouts  1.59 us (3%)
  between operations  0.64 us (1%)
    pallas_call x1, Pallas kernels, local(): pl.pallas_call(functools.partial(kernel, nums), out_shape=(pltpu.VMEM(den...  50.2 us
    unnamed x2, local copies, waits for them, and re-layouts  1.59 us

profile of v6, /device:TPU:1, one launch (start us, length us, event | category | flops | bytes accessed | tf_op | source)
XLA Modules:
  0.0 52.4 jit_solution(17587916709229594238)
XLA Ops:
  0.6 50.2 %cycle.1 = (f32[16,16,1024]{2,1,0:T(8,128)S(1)}, f32[64,64]{1,0:T(8,128)S(1)}) custom-call(f32[16,16,1024]{2,1,0:T(8,128)} %dens.1), custom_call_target="tpu_custom_call" | custom-call | tf_op jit(solution)/shard_map/cycle/pallas_call | solution.py:627
  50.8 1.0 %copy.5 = f32[16,16,1024]{2,1,0:T(8,128)} copy(f32[16,16,1024]{2,1,0:T(8,128)S(1)} %get-tuple-element.2) | data formatting | bytes 2097152
  51.8 0.6 %copy.6 = f32[64,64]{1,0:T(8,128)} copy(f32[64,64]{1,0:T(8,128)S(1)} %get-tuple-element.3) | data formatting | bytes 32768
